TPU v7x, 128 devices: a whole 4x4x4 slice. The times are simulated.
128 devices in a mesh: dp: 1, sp: 128 (over z, y, x, core).
Axes of the slice: x: 4, y: 4, z: 4, core: 2. Of those that a mesh axis runs over, the one named last changes fastest.
Arguments:
- x_patch: bfloat16 [32, 16384, 512], P('dp', 'sp')
- w_tok1: bfloat16 [16384, 256], P('sp')
- b_tok1: float32 [256], P('sp')
- w_tok2: bfloat16 [256, 16384], P(None, 'sp')
- b_tok2: float32 [16384], P('sp')
- w_ch1: bfloat16 [512, 2048], replicated
- b_ch1: float32 [2048], replicated
- w_ch2: bfloat16 [2048, 512], replicated
- b_ch2: float32 [512], replicated
- ln1_gain: float32 [512], replicated
- ln1_bias: float32 [512], replicated
- ln2_gain: float32 [512], replicated
- ln2_bias: float32 [512], replicated
Outputs:
- output: bfloat16 [32, 16384, 512], P('dp', 'sp')
All inputs are finite; a program needn't handle non-finite values.
Results may differ from a plain program's by a relative error of at most 0.00982353.
Values are sent between devices in bfloat16 or wider.
A program may use at most 1 GiB of HBM per device.

v0:
```python
import jax
import jax.numpy as jnp
from jax import lax
from jax.sharding import PartitionSpec as P

LN_EPS = 1e-6


def layer_norm(values, ln_gain, ln_bias):
    mean_val = jnp.mean(values, axis=-1, keepdims=True)
    centred = values - mean_val
    var_val = jnp.mean(centred * centred, axis=-1, keepdims=True)
    return centred * lax.rsqrt(var_val + LN_EPS) * ln_gain + ln_bias


def channel_mix(x_mid, w_ch1, b_ch1, w_ch2, b_ch2, ln2_gain, ln2_bias):
    mid_wide = x_mid.astype(jnp.float32)
    normed_two = layer_norm(mid_wide, ln2_gain, ln2_bias).astype(jnp.bfloat16)
    ch_pre = jnp.einsum("bsc,cf->bsf", normed_two, w_ch1, preferred_element_type=jnp.float32) + b_ch1
    ch_act = jax.nn.gelu(ch_pre).astype(jnp.bfloat16)
    ch_out = jnp.einsum("bsf,fc->bsc", ch_act, w_ch2, preferred_element_type=jnp.float32) + b_ch2
    return (mid_wide + ch_out).astype(jnp.bfloat16)


def solution(mesh):
    row_spec = P("dp", "sp", None)

    def local_layer(x_blk, w1_rows, b1_part, w2_cols, b2_part, w_ch1, b_ch1, w_ch2, b_ch2, ln1_gain, ln1_bias, ln2_gain, ln2_bias):
        x_wide = x_blk.astype(jnp.float32)
        normed = layer_norm(x_wide, ln1_gain, ln1_bias).astype(jnp.bfloat16)
        part_pre = jnp.einsum("bsc,sd->bdc", normed, w1_rows, preferred_element_type=jnp.float32)
        tok_pre = lax.psum_scatter(part_pre, "sp", scatter_dimension=1, tiled=True) + b1_part[None, :, None]
        tok_act = jax.nn.gelu(tok_pre).astype(jnp.bfloat16)
        act_full = lax.all_gather(tok_act, "sp", axis=1, tiled=True)
        tok_out = jnp.einsum("bdc,ds->bsc", act_full, w2_cols, preferred_element_type=jnp.float32) + b2_part[None, :, None]
        x_mid = (x_wide + tok_out).astype(jnp.bfloat16)
        return channel_mix(x_mid, w_ch1, b_ch1, w_ch2, b_ch2, ln2_gain, ln2_bias)

    in_specs = (row_spec, P("sp", None), P("sp"), P(None, "sp"), P("sp"), P(None, None), P(None), P(None, None), P(None), P(None), P(None), P(None), P(None))
    return jax.shard_map(local_layer, mesh=mesh, in_specs=in_specs, out_specs=row_spec, check_vma=False)
```

profile of v0, /device:TPU:1, one launch (start us, length us, event | category | flops | bytes accessed | tf_op | source)
XLA Modules:
  0.0 853.8 jit_solution(11312374767610570776)
XLA Ops:
  6.5 0.0 copy-start
  6.5 0.0 reduce-scatter.2.cloned.1.call-start
  6.6 6.6 copy.19
  13.1 3.0 convert_reduce_fusion.1
  16.2 3.5 fusion.16
  19.6 0.0 copy-done.4
  19.7 0.0 copy-done.5
  19.7 0.0 copy-done.3
  19.7 8.2 convolution_bitcast_fusion
  27.9 20.2 %copy.20 = f32[32,256,512]{2,0,1:T(8,128)} copy(f32[32,256,512]{1,2,0:T(8,128)} %convolution_bitcast_fusion) | data formatting | bytes 33554432 | tf_op jit(solution)/shard_map/bsc,sd->bdc/transpose | solution.py:31
  48.0 0.0 reduce-scatter.2.cloned.1.call-update
  48.0 0.2 all-gather.2.cloned.1.call-start
  48.3 668.4 %reduce-scatter.2.cloned.1.call-done = f32[32,2,512]{2,0,1:T(8,128)} async-done(((f32[32,256,512]{2,0,1:T(8,128)}), f32[32,2,512]{2,0,1:T(8,128)}) %reduce-scatter.2.cloned.1.call-update) | async-done | bytes 131088 | tf_op jit(solution)/shard_map/reduce_scatter | solution.py:32
  716.7 1.7 fusion.49
  718.4 0.0 all-gather.2.cloned.1.call-update
  718.4 0.0 copy-start.9
  718.4 0.0 copy-start.10
  718.4 0.0 copy-start.11
  718.4 71.8 %all-gather.2.cloned.1.call-done = bf16[32,256,512]{2,0,1:T(8,128)(2,1)} async-done(((bf16[32,2,512]{2,0,1:T(8,128)(2,1)}), bf16[32,256,512]{2,0,1:T(8,128)(2,1)}) %all-gather.2.cloned.1.call-update) | async-done | bytes 8388624 | tf_op jit(solution)/shard_map/all_gather | solution.py:34
  790.2 0.0 copy-done.13
  790.2 15.1 %convert_reduce_fusion = (f32[32,128]{1,0:T(8,128)S(1)}, bf16[32,128,512]{1,2,0:T(8,128)(2,1)S(1)}) fusion(f32[128]{0:T(128)S(1)} %copy-done.13, bf16[256,128]{1,0:T(8,128)(2,1)S(1)} %copy-done.8, bf16[32,256,512]{2,0,1:T(8,128)(2,1)} %all-gather.2.cloned.1.call-done, bf16[32,128,512]{1,2,0:T(8,128)(2,1)} %copy.19), kind=kOutput, calls=%fused_computation.11 | convolution fusion | flops 1086320640 | bytes 16859648 | tf_op jit(solution)/shard_map/bdc,ds->bsc/dot_general | solution.py:35
  805.3 1.5 fusion.12
  806.8 0.0 copy-done
  806.8 0.0 copy-done.9
  806.9 0.0 copy-done.10
  806.9 0.0 copy-done.11
  806.9 0.0 copy-start.7
  806.9 0.0 copy-start.12
  806.9 20.6 %fusion.7.clone.4 = bf16[32,128,2048]{2,1,0:T(8,128)(2,1)} fusion(f32[2048]{0:T(1024)S(1)} %copy-done.9, bf16[32,128,512]{1,2,0:T(8,128)(2,1)S(1)} %get-tuple-element.6, f32[512]{0:T(512)S(1)} %copy-done.10, f32[512]{0:T(512)S(1)} %copy-done.11, f32[32,128]{1,0:T(8,128)S(1)} %add_rsqrt_fusion, f32[32,128]{1,0:T(8,128)S(1)} %broadcast_multiply_fusion, ...), kind=kOutput, calls=%fused_computation.8.clone.clone.clone.1 | convolution fusion | flops 8686403584 | bytes 23113728 | tf_op jit(solution)/shard_map/bsc,cf->bsf/dot_general | solution.py:19
  827.5 0.0 copy-done.12
  827.5 13.1 %fusion.21 = bf16[32,128,512]{1,2,0:T(8,128)(2,1)} fusion(bf16[32,128,512]{1,2,0:T(8,128)(2,1)S(1)} %get-tuple-element.6, f32[512]{0:T(512)S(1)} %copy-done.12, bf16[2048,512]{1,0:T(8,128)(2,1)S(1)} %copy-done.7, bf16[32,128,2048]{2,1,0:T(8,128)(2,1)} %fusion.7.clone.4), kind=kOutput, calls=%fused_computation.29 | convolution fusion | flops 8598323200 | bytes 27265024 | tf_op jit(solution)/shard_map/bsf,fc->bsc/dot_general | solution.py:21
  840.6 6.4 copy.24
  (17 shorter events, 0.0 us)
Async XLA Ops:
  6.5 800.3 %copy-start = (bf16[512,2048]{1,0:T(8,128)(2,1)S(1)}, bf16[512,2048]{1,0:T(8,128)(2,1)}, u32[]{:S(2)}) copy-start(bf16[512,2048]{1,0:T(8,128)(2,1)} %param.18) | copy-start | bytes 6291460
  6.5 13.1 %copy-start.4 = (f32[512]{0:T(512)S(1)}, f32[512]{0:T(512)}, u32[]{:S(2)}) copy-start(f32[512]{0:T(512)} %param.23) | copy-start | bytes 6148
  6.5 13.1 %copy-start.5 = (f32[512]{0:T(512)S(1)}, f32[512]{0:T(512)}, u32[]{:S(2)}) copy-start(f32[512]{0:T(512)} %param.22) | copy-start | bytes 6148
  6.5 13.1 %copy-start.3 = (bf16[128,256]{1,0:T(8,128)(2,1)S(1)}, bf16[128,256]{1,0:T(8,128)(2,1)}, u32[]{:S(2)}) copy-start(bf16[128,256]{1,0:T(8,128)(2,1)} %param.14) | copy-start | bytes 196612
  6.5 710.2 %reduce-scatter.2.cloned.1.call-start = ((), (), s32[]{:S(2)}) async-start(), calls=%async_computation.1 | async-start | bytes 16908288 | tf_op jit(solution)/shard_map/reduce_scatter | solution.py:32
  13.1 6.5 copy-start.2
  48.0 668.7 %copy-start.6 = (f32[2]{0:T(128)S(1)}, f32[2]{0:T(128)}, u32[]{:S(2)}) copy-start(f32[2]{0:T(128)} %param.15) | copy-start | bytes 28
  48.0 742.2 %copy-start.8 = (bf16[256,128]{1,0:T(8,128)(2,1)S(1)}, bf16[256,128]{1,0:T(8,128)(2,1)}, u32[]{:S(2)}) copy-start(bf16[256,128]{1,0:T(8,128)(2,1)} %param.16) | copy-start | bytes 196612
  48.0 742.2 %copy-start.13 = (f32[128]{0:T(128)S(1)}, f32[128]{0:T(128)}, u32[]{:S(2)}) copy-start(f32[128]{0:T(128)} %param.17) | copy-start | bytes 1540
  48.0 742.2 %all-gather.2.cloned.1.call-start = ((), (), s32[]{:S(2)}) async-start(), calls=%async_computation.2 | async-start | bytes 8454144 | tf_op jit(solution)/shard_map/all_gather | solution.py:34
  718.4 88.4 %copy-start.9 = (f32[2048]{0:T(1024)S(1)}, f32[2048]{0:T(1024)}, u32[]{:S(2)}) copy-start(f32[2048]{0:T(1024)} %param.19) | copy-start | bytes 24580
  718.4 88.4 %copy-start.10 = (f32[512]{0:T(512)S(1)}, f32[512]{0:T(512)}, u32[]{:S(2)}) copy-start(f32[512]{0:T(512)} %param.25) | copy-start | bytes 6148
  718.4 88.4 %copy-start.11 = (f32[512]{0:T(512)S(1)}, f32[512]{0:T(512)}, u32[]{:S(2)}) copy-start(f32[512]{0:T(512)} %param.24) | copy-start | bytes 6148
  806.9 20.6 %copy-start.7 = (bf16[2048,512]{1,0:T(8,128)(2,1)S(1)}, bf16[2048,512]{1,0:T(8,128)(2,1)}, u32[]{:S(2)}) copy-start(bf16[2048,512]{1,0:T(8,128)(2,1)} %param.20) | copy-start | bytes 6291460
  806.9 20.6 %copy-start.12 = (f32[512]{0:T(512)S(1)}, f32[512]{0:T(512)}, u32[]{:S(2)}) copy-start(f32[512]{0:T(512)} %param.21) | copy-start | bytes 6148
  827.5 19.5 %copy-start.1 = (bf16[512,2048]{1,0:T(8,128)(2,1)S(1)}, bf16[512,2048]{1,0:T(8,128)(2,1)}, u32[]{:S(2)}) copy-start(bf16[512,2048]{1,0:T(8,128)(2,1)} %param.18) | copy-start | bytes 6291460
Sparse Core Ops, SparseCore 0:
  48.2 668.4 reduce-scatter.1
  719.7 70.4 all-gather.1
where the time goes:
time: 855 us; the launch traced here: 854 us
  waiting for transfers between devices  740 us (87%)
  matrix products  56.9 us (7%)
  local copies, waits for them, and re-layouts  33.2 us (4%)
  between operations  13.6 us (2%)
  other arithmetic  9.62 us (1%)
    reduce_scatter x1, waiting for transfers between devices, local_layer(): lax.psum_scatter(part_pre, 'sp', scatter_dimension=1, tiled=True)  668 us
    all_gather x1, waiting for transfers between devices, local_layer(): act_full = lax.all_gather(tok_act, 'sp', axis=1, tiled=True)  71.8 us
    dot_general x1, matrix products, channel_mix(): jnp.einsum('bsc,cf->bsf', normed_two, w_ch1, preferred_element_type=jnp.f...  20.6 us
    transpose x1, local copies, waits for them, and re-layouts, local_layer(): jnp.einsum('bsc,sd->bdc', normed, w1_rows, preferred_element_type=jnp.flo...  20.2 us
  transfers between devices with their start and end apart: 2, of which 2 were waited for; matrix products, arithmetic and copies ran while one was open for 0% of the time, Pallas kernels for 0%

commit v1 on v0

v1 whole, which is shorter than its diff:
```python
import functools

import jax
import jax.numpy as jnp
from jax import lax
from jax.experimental import pallas as pl
from jax.experimental.pallas import tpu as pltpu
from jax.sharding import PartitionSpec as P

LN_EPS = 1e-6
F32 = jnp.float32
BF16 = jnp.bfloat16
HALF = (pl.ds(0, 256), pl.ds(256, 256))
CHUNKS = (
    ("xyz", "yzx"),
    ("yzx", "zxy"),
    ("zxy", "xyz"),
    ("xyz", "xzy"),
)
K = len(CHUNKS)


def layer_norm(values, ln_gain, ln_bias):
    mean_val = jnp.mean(values, axis=-1, keepdims=True)
    centred = values - mean_val
    var_val = jnp.mean(centred * centred, axis=-1, keepdims=True)
    return centred * lax.rsqrt(var_val + LN_EPS) * ln_gain + ln_bias


def gelu(a):
    return 0.5 * a * (1.0 + jnp.tanh(0.7978845608028654 * (a + 0.044715 * (a * a * a))))


def token_kernel(
    x_hbm, w1_ref, b1_ref, gain_ref, bias_ref, g_hbm,
    xv, w1o, w1t, tile_in, tile_all, usend, ustage, uall, relay, hb, rq0, rd0, rs0, hq, rq1, rd1, rs1, gall,
    send_sems, recv_sems, local_sems,
):
    me = lax.axis_index("sp")
    co = {"z": me // 32, "y": (me // 8) % 4, "x": (me // 2) % 4}
    core = me % 2
    other = 1 - core

    def device(c=None, **at):
        z, y, x = (at.get(a, co[a]) for a in "zyx")
        return ((z * 4 + y) * 4 + x) * 2 + (core if c is None else c)

    def near(axis, step):
        return device(**{axis: (co[axis] + step) % 4})

    sent = []

    def send(src, dst, to):
        n = len(sent)
        copy = pltpu.make_async_remote_copy(
            src_ref=src, dst_ref=dst, send_sem=send_sems.at[n], recv_sem=recv_sems.at[n],
            device_id={"sp": to}, device_id_type=pl.DeviceIdType.MESH,
        )
        copy.start()
        sent.append(copy)
        return copy

    loads = []
    for k in range(K):
        load = pltpu.make_async_copy(x_hbm.at[pl.ds(8 * k, 8)], xv.at[pl.ds(8 * k, 8)], local_sems.at[k])
        load.start()
        loads.append(load)

    partner = device(c=other)
    group = [device(c=(core + j) % 2, x=(co["x"] + s) % 4) for s in range(4) for j in range(2) if (s, j) != (0, 0)]
    peers = group + [near(a, s) for a in "yz" for s in (1, 2, 3)]
    barrier = pltpu.get_barrier_semaphore()
    for peer in peers:
        pl.semaphore_signal(barrier, inc=1, device_id={"sp": peer}, device_id_type=pl.DeviceIdType.MESH)
    pl.semaphore_wait(barrier, len(peers))

    w1o[...] = w1_ref[...].T
    w1_in = {}
    def lanes(pos, c):
        return pl.ds(pl.multiple_of((pos * 2 + c) * 128, 128), 128)
    for i, a in enumerate("xyz"):
        w1t[i, :, lanes(co[a], core)] = w1o[...]
        dst = w1t.at[i, :, lanes(co[a], core)]
        w1_in[a] = [send(w1o, dst, near(a, s)) for s in (1, 2, 3)] + [send(w1o, dst, partner)]

    row = lax.broadcasted_iota(jnp.int32, (16, 128), 0)
    slot = co["x"] * 2 + core
    tile_in[8] = jnp.where(row == 2 * slot, b1_ref[0], jnp.where(row == 2 * slot + 1, b1_ref[1], 0.0))
    tile_in[slot] = tile_in[8]
    b1_in = [send(tile_in.at[8], tile_in.at[slot], to) for to in group]

    gain, bias = gain_ref[...], bias_ref[...]
    pairs = []

    def norm(k):
        loads[k].wait()

        def body(i, carry):
            mine = layer_norm(xv[8 * k + 4 * core + i].astype(F32), gain, bias).astype(BF16)
            ustage[k, i, core] = mine
            theirs = layer_norm(xv[8 * k + 4 * other + i].astype(F32), gain, bias).astype(BF16)
            usend[k, i] = theirs
            return carry

        lax.fori_loop(0, 4, body, 0)
        return send(usend.at[k], ustage.at[k, :, core], partner)

    def exchange(k, pair):
        pair.wait_recv()
        a = CHUNKS[k][0][0]
        p = co[a]
        right, left = near(a, 1), near(a, 3)
        opp, rt, lf = (p + 2) % 4, (p + 1) % 4, (p + 3) % 4
        passing = [
            send(ustage.at[k, opp, :, :, HALF[0]], relay.at[k, 0], right),
            send(ustage.at[k, opp, :, :, HALF[1]], relay.at[k, 1], left),
        ]
        direct = [
            send(ustage.at[k, rt], uall.at[k, p], right),
            send(ustage.at[k, lf], uall.at[k, p], left),
        ]
        uall[k, p] = ustage[k, p]
        return passing, direct

    def pass_on(k, state):
        passing, direct = state
        a = CHUNKS[k][0][0]
        p = co[a]
        passing[0].wait_recv()
        direct.append(send(relay.at[k, 0], uall.at[k, (p + 3) % 4, :, :, HALF[0]], near(a, 1)))
        passing[1].wait_recv()
        direct.append(send(relay.at[k, 1], uall.at[k, (p + 1) % 4, :, :, HALF[1]], near(a, 3)))
        return direct

    def ring_first(a, part, in_opp, in_near):
        q = co[a]
        right, left = near(a, 1), near(a, 3)
        opp, rt, lf = (q + 2) % 4, (q + 1) % 4, (q + 3) % 4
        first = [send(part(opp, HALF[0]), in_opp.at[0], right), send(part(opp, HALF[1]), in_opp.at[1], left)]
        straight = [send(part(rt, HALF[1]), in_near.at[0], right), send(part(lf, HALF[0]), in_near.at[1], left)]
        return first, straight

    def ring_second(a, part, in_opp, in_sum, first):
        q = co[a]
        right, left = near(a, 1), near(a, 3)
        rt, lf = (q + 1) % 4, (q + 3) % 4
        out = []
        for j, (pos, to) in enumerate(((rt, right), (lf, left))):
            first[j].wait_recv()
            ref = part(pos, HALF[j])
            ref[...] = ref[...] + in_opp[j]
            out.append(send(ref, in_sum.at[j], to))
        return out

    def ring_last(a, part, in_near, in_sum, straight, second):
        q = co[a]
        for copy in straight + second:
            copy.wait_recv()
        low = part(q, HALF[0])[...] + in_near[1] + in_sum[0]
        high = part(q, HALF[1])[...] + in_near[0] + in_sum[1]
        return low, high

    def part_q(k):
        return lambda pos, half: hb.at[k, :, pos, :, half]

    def part_r(k):
        return lambda pos, half: hq.at[k, pos, :, half]

    def mix(k, direct):
        for copy in direct:
            copy.wait_recv()
        axes = CHUNKS[k][0]
        u = uall[k].reshape(1024, 512)
        part = jnp.dot(w1t["xyz".index(axes[0])], u, preferred_element_type=F32)
        hb[k] = part.reshape(4, 4, 16, 512)
        return ring_first(axes[1], part_q(k), rq0.at[k], rd0.at[k])

    def sum_q(k, state):
        first, straight = state
        return straight, ring_second(CHUNKS[k][0][1], part_q(k), rq0.at[k], rs0.at[k], first)

    def start_r(k, state):
        axes = CHUNKS[k][0]
        low, high = ring_last(axes[1], part_q(k), rd0.at[k], rs0.at[k], *state)
        hq[k, :, :, HALF[0]] = low
        hq[k, :, :, HALF[1]] = high
        return ring_first(axes[2], part_r(k), rq1.at[k], rd1.at[k])

    def sum_r(k, state):
        first, straight = state
        return straight, ring_second(CHUNKS[k][0][2], part_r(k), rq1.at[k], rs1.at[k], first)

    def block(k, known):
        at = [slice(None) if a in known else co[a] for a in (CHUNKS[k][0][0], CHUNKS[k][0][2], CHUNKS[k][0][1])]
        return lambda axis=None, pos=None, half=slice(None): gall.at[
            (k, core) + tuple(pos if a == axis else v for a, v in zip(CHUNKS[k][0][0] + CHUNKS[k][0][2] + CHUNKS[k][0][1], at))
            + (slice(None), half)
        ]

    def activate(k, state):
        axes = CHUNKS[k][0]
        low, high = ring_last(axes[2], part_r(k), rd1.at[k], rs1.at[k], *state)
        tile = tile_all[co[axes[2]], co[axes[1]]]
        shift = jnp.concatenate([tile, tile], axis=1)
        where = (k, core, co[axes[0]], co[axes[2]], co[axes[1]])
        gall[where + (slice(None), HALF[0])] = gelu(low + shift).astype(BF16)
        gall[where + (slice(None), HALF[1])] = gelu(high + shift).astype(BF16)
        a = CHUNKS[k][1][0]
        own = block(k, "")()
        return [send(own, own, near(a, s)) for s in (1, 3, 2)]

    def gather(k, n, waits):
        for copy in waits:
            copy.wait_recv()
        a = CHUNKS[k][1][n]
        own = block(k, CHUNKS[k][1][:n])()
        return [send(own, own, near(a, 1)), send(own, own, near(a, 3))]

    def gather_on(k, n, waits):
        a = CHUNKS[k][1][n]
        at = block(k, CHUNKS[k][1][:n])
        out = list(waits)
        for j, (pos, to) in enumerate((((co[a] + 3) % 4, near(a, 1)), ((co[a] + 1) % 4, near(a, 3)))):
            waits[j].wait_recv()
            ref = at(a, pos, HALF[j])
            out.append(send(ref, ref, to))
        return out[2:]

    def share(k, waits):
        for copy in waits:
            copy.wait_recv()
        return send(gall.at[k, core], gall.at[k, core], partner)

    def write(k, copy):
        copy.wait_recv()
        out = pltpu.make_async_copy(gall.at[k], g_hbm.at[k], local_sems.at[K + k])
        out.start()
        return out

    state = [norm(k) for k in range(K)]
    state = [exchange(k, s) for k, s in enumerate(state)]

    for copy in b1_in:
        copy.wait_recv()
    tile = tile_in[0]
    for j in range(1, 8):
        tile = tile + tile_in[j]
    tile_all[co["z"], co["y"]] = tile
    ref = tile_all.at[co["z"], co["y"]]
    b1_in = [send(ref, ref, near("y", s)) for s in (1, 2, 3)]
    w1_share = []
    for i, a in enumerate("xyz"):
        for s, copy in zip((3, 2, 1), w1_in[a]):
            copy.wait_recv()
            ref = w1t.at[i, :, lanes((co[a] + s) % 4, core)]
            w1_share.append(send(ref, ref, partner))
        w1_share.append(w1_in[a][3])
    for copy in b1_in:
        copy.wait_recv()
    ref = tile_all.at[co["z"]]
    b1_in = [send(ref, ref, near("z", s)) for s in (1, 2, 3)]
    for copy in w1_share + b1_in:
        copy.wait_recv()

    for step in (pass_on, mix, sum_q, start_r, sum_r, activate):
        state = [step(k, s) for k, s in enumerate(state)]
    for n in (1, 2):
        state = [gather(k, n, s) for k, s in enumerate(state)]
        state = [gather_on(k, n, s) for k, s in enumerate(state)]
    state = [share(k, s) for k, s in enumerate(state)]
    state = [write(k, s) for k, s in enumerate(state)]
    for copy in state:
        copy.wait()
    for copy in sent:
        copy.wait_send()


N_COPIES = 31 * K + 12 + 7 + 3 + 9 + 3


def token_hidden(x, w1, b1, gain, bias):
    any_space = pl.BlockSpec(memory_space=pl.ANY)
    vmem = pl.BlockSpec(memory_space=pltpu.VMEM)
    out = pl.pallas_call(
        token_kernel,
        name="token_hidden",
        out_shape=jax.ShapeDtypeStruct((K, 2, 4, 4, 4, 16, 512), BF16),
        in_specs=[any_space, vmem, pl.BlockSpec(memory_space=pltpu.SMEM), vmem, vmem],
        out_specs=any_space,
        scratch_shapes=[
            pltpu.VMEM((32, 128, 512), BF16),
            pltpu.VMEM((256, 128), BF16),
            pltpu.VMEM((3, 256, 1024), BF16),
            pltpu.VMEM((9, 16, 128), F32),
            pltpu.VMEM((4, 4, 16, 128), F32),
            pltpu.VMEM((K, 4, 128, 512), BF16),
            pltpu.VMEM((K, 4, 2, 128, 512), BF16),
            pltpu.VMEM((K, 4, 2, 128, 512), BF16),
            pltpu.VMEM((K, 2, 2, 128, 256), BF16),
            pltpu.VMEM((K, 4, 4, 16, 512), F32),
            pltpu.VMEM((K, 2, 4, 16, 256), F32),
            pltpu.VMEM((K, 2, 4, 16, 256), F32),
            pltpu.VMEM((K, 2, 4, 16, 256), F32),
            pltpu.VMEM((K, 4, 16, 512), F32),
            pltpu.VMEM((K, 2, 16, 256), F32),
            pltpu.VMEM((K, 2, 16, 256), F32),
            pltpu.VMEM((K, 2, 16, 256), F32),
            pltpu.VMEM((K, 2, 4, 4, 4, 16, 512), BF16),
            pltpu.SemaphoreType.DMA((N_COPIES,)),
            pltpu.SemaphoreType.DMA((N_COPIES,)),
            pltpu.SemaphoreType.DMA((2 * K,)),
        ],
        compiler_params=pltpu.CompilerParams(
            collective_id=0, has_side_effects=True, vmem_limit_bytes=60 * 1024 * 1024
        ),
    )(x, w1, b1, gain.reshape(1, 512), bias.reshape(1, 512))
    return out.reshape(32, 256, 512)


def channel_mix(x_mid, w_ch1, b_ch1, w_ch2, b_ch2, ln2_gain, ln2_bias):
    mid_wide = x_mid.astype(jnp.float32)
    normed_two = layer_norm(mid_wide, ln2_gain, ln2_bias).astype(jnp.bfloat16)
    ch_pre = jnp.einsum("bsc,cf->bsf", normed_two, w_ch1, preferred_element_type=jnp.float32) + b_ch1
    ch_act = jax.nn.gelu(ch_pre).astype(jnp.bfloat16)
    ch_out = jnp.einsum("bsf,fc->bsc", ch_act, w_ch2, preferred_element_type=jnp.float32) + b_ch2
    return (mid_wide + ch_out).astype(jnp.bfloat16)


def solution(mesh):
    row_spec = P("dp", "sp", None)

    def local_layer(x_blk, w1_rows, b1_part, w2_cols, b2_part, w_ch1, b_ch1, w_ch2, b_ch2, ln1_gain, ln1_bias, ln2_gain, ln2_bias):
        act_full = token_hidden(x_blk, w1_rows, b1_part, ln1_gain, ln1_bias)
        tok_out = jnp.einsum("bdc,ds->bsc", act_full, w2_cols, preferred_element_type=jnp.float32) + b2_part[None, :, None]
        x_mid = (x_blk.astype(jnp.float32) + tok_out).astype(jnp.bfloat16)
        return channel_mix(x_mid, w_ch1, b_ch1, w_ch2, b_ch2, ln2_gain, ln2_bias)

    in_specs = (row_spec, P("sp", None), P("sp"), P(None, "sp"), P("sp"), P(None, None), P(None), P(None, None), P(None), P(None), P(None), P(None), P(None))
    return jax.shard_map(local_layer, mesh=mesh, in_specs=in_specs, out_specs=row_spec, check_vma=False)
```

time: 855 us -> 143 us (0.17)
  waiting for transfers between devices: 740 us -> 0 us
  Pallas kernels: 0 us -> 87.2 us
  local copies, waits for them, and re-layouts: 33.2 us -> 13 us
  matrix products: 56.9 us -> 40.6 us
  between operations: 13.6 us -> 0.13 us
    reduce_scatter x1 -> x0, waiting for transfers between devices: 668 us -> none  [local_layer(): lax.psum_scatter(part_pre, 'sp', scatter_dimension=1, tiled=True)]
    pallas_call x0 -> x1, Pallas kernels: none -> 87.2 us  [token_hidden(): pl.pallas_call(token_kernel, name='token_hidden', out_shape=jax.ShapeDtyp...]
    all_gather x1 -> x0, waiting for transfers between devices: 71.8 us -> none  [local_layer(): act_full = lax.all_gather(tok_act, 'sp', axis=1, tiled=True)]
    transpose x1 -> x0, local copies, waits for them, and re-layouts: 20.2 us -> none  [local_layer(): jnp.einsum('bsc,sd->bdc', normed, w1_rows, preferred_element_type=jnp.flo...]
  transfers between devices with their start and end apart: 2 -> 0, of which waited for: 2 -> 0; matrix products, arithmetic and copies ran while one was open for 0% -> 0% of each run, Pallas kernels for 0% -> 0%
where the time goes in v1:
time: 143 us; the launch traced here: 142 us
  Pallas kernels  87.2 us (61%)
  matrix products  40.6 us (28%)
  local copies, waits for them, and re-layouts  13 us (9%)
    pallas_call x1, Pallas kernels, token_hidden(): pl.pallas_call(token_kernel, name='token_hidden', out_shape=jax.ShapeDtyp...  87.2 us
    dot_general x1, matrix products, channel_mix(): jnp.einsum('bsc,cf->bsf', normed_two, w_ch1, preferred_element_type=jnp.f...  20.7 us
    dot_general x1, matrix products, channel_mix(): jnp.einsum('bsf,fc->bsc', ch_act, w_ch2, preferred_element_type=jnp.float32)  12.9 us
    dot_general x1, matrix products, local_layer(): jnp.einsum('bdc,ds->bsc', act_full, w2_cols, preferred_element_type=jnp.f...  7 us
    unnamed x17, local copies, waits for them, and re-layouts  6.59 us
    convert_element_type x1, local copies, waits for them, and re-layouts, channel_mix(): return (mid_wide + ch_out).astype(jnp.bfloat16)  6.41 us

profile of v1, /device:TPU:1, one launch (start us, length us, event | category | flops | bytes accessed | tf_op | source)
XLA Modules:
  0.0 142.2 jit_solution(343755419899333834)
XLA Ops:
  0.0 0.0 copy-start
  0.0 6.5 %copy.14 = bf16[32,128,512]{1,2,0:T(8,128)(2,1)} copy(bf16[32,128,512]{2,1,0:T(8,128)(2,1)} %x_hbm.1) | data formatting | bytes 8388608 | tf_op args[0]
  6.6 0.0 copy-start.2
  6.6 0.0 copy-start.7
  6.6 87.2 %token_hidden.1 = bf16[4,2,4,4,4,16,512]{6,5,4,3,2,1,0:T(8,128)(2,1)} custom-call(bf16[32,128,512]{2,1,0:T(8,128)(2,1)} %x_hbm.1, bf16[128,256]{1,0:T(8,128)(2,1)} %w1_ref.1, f32[2]{0:T(128)} %b1_ref.1, f32[1,512]{1,0:T(1,128)} %bitcast.27, f32[1,512]{1,0:T(1,128)} %bitcast.28), custom_call_target="tpu_custom_call" | custom-call | tf_op jit(solution)/shard_map/token_hidden/pallas_call | solution.py:284
  93.7 0.0 copy-done.2
  93.8 0.0 copy-done.7
  93.8 0.0 copy-start.3
  93.8 0.0 copy-start.4
  93.8 0.0 copy-start.5
  93.8 7.0 %convert_reduce_fusion = (f32[32,128]{1,0:T(8,128)S(1)}, bf16[32,128,512]{1,2,0:T(8,128)(2,1)S(1)}) fusion(f32[128]{0:T(128)S(1)} %copy-done.7, bf16[32,256,512]{2,1,0:T(8,128)(2,1)} %bitcast.26, bf16[256,128]{1,0:T(8,128)(2,1)S(1)} %copy-done.2, bf16[32,128,512]{1,2,0:T(8,128)(2,1)} %copy.14), kind=kOutput, calls=%fused_computation.11 | convolution fusion | flops 1086320640 | bytes 16859648 | tf_op jit(solution)/shard_map/bdc,ds->bsc/dot_general | solution.py:334
  100.8 1.3 fusion.10
  102.1 0.0 copy-done
  102.1 0.0 copy-done.3
  102.1 0.0 copy-done.4
  102.1 0.0 copy-done.5
  102.1 0.0 copy-start.1
  102.1 0.0 copy-start.6
  102.2 20.7 %fusion.7.clone.4 = bf16[32,128,2048]{2,1,0:T(8,128)(2,1)} fusion(f32[2048]{0:T(1024)S(1)} %copy-done.3, bf16[32,128,512]{1,2,0:T(8,128)(2,1)S(1)} %get-tuple-element.6, f32[512]{0:T(512)S(1)} %copy-done.4, f32[512]{0:T(512)S(1)} %copy-done.5, f32[32,128]{1,0:T(8,128)S(1)} %add_rsqrt_fusion, f32[32,128]{1,0:T(8,128)S(1)} %broadcast_multiply_fusion, ...), kind=kOutput, calls=%fused_computation.8.clone.clone.clone.1 | convolution fusion | flops 8686403584 | bytes 23113728 | tf_op jit(solution)/shard_map/bsc,cf->bsf/dot_general | solution.py:323
  122.9 0.0 copy-done.1
  122.9 0.0 copy-done.6
  122.9 12.9 %fusion.14 = bf16[32,128,512]{1,2,0:T(8,128)(2,1)} fusion(bf16[32,128,512]{1,2,0:T(8,128)(2,1)S(1)} %get-tuple-element.6, f32[512]{0:T(512)S(1)} %copy-done.6, bf16[2048,512]{1,0:T(8,128)(2,1)S(1)} %copy-done.1, bf16[32,128,2048]{2,1,0:T(8,128)(2,1)} %fusion.7.clone.4), kind=kOutput, calls=%fused_computation.18 | convolution fusion | flops 8598323200 | bytes 27265024 | tf_op jit(solution)/shard_map/bsf,fc->bsc/dot_general | solution.py:325
  135.8 6.4 %copy.18 = bf16[32,128,512]{2,1,0:T(8,128)(2,1)} copy(bf16[32,128,512]{1,2,0:T(8,128)(2,1)} %fusion.14) | data formatting | bytes 8388608 | tf_op jit(solution)/shard_map/convert_element_type | solution.py:326
  (2 shorter events, 0.0 us)
Async XLA Ops:
  0.0 102.1 %copy-start = (bf16[512,2048]{1,0:T(8,128)(2,1)S(1)}, bf16[512,2048]{1,0:T(8,128)(2,1)}, u32[]{:S(2)}) copy-start(bf16[512,2048]{1,0:T(8,128)(2,1)} %param.18) | copy-start | bytes 6291460
  6.6 87.2 %copy-start.2 = (bf16[256,128]{1,0:T(8,128)(2,1)S(1)}, bf16[256,128]{1,0:T(8,128)(2,1)}, u32[]{:S(2)}) copy-start(bf16[256,128]{1,0:T(8,128)(2,1)} %param.16) | copy-start | bytes 196612
  6.6 87.2 %copy-start.7 = (f32[128]{0:T(128)S(1)}, f32[128]{0:T(128)}, u32[]{:S(2)}) copy-start(f32[128]{0:T(128)} %param.17) | copy-start | bytes 1540
  93.8 8.3 %copy-start.3 = (f32[2048]{0:T(1024)S(1)}, f32[2048]{0:T(1024)}, u32[]{:S(2)}) copy-start(f32[2048]{0:T(1024)} %param.19) | copy-start | bytes 24580
  93.8 8.3 %copy-start.4 = (f32[512]{0:T(512)S(1)}, f32[512]{0:T(512)}, u32[]{:S(2)}) copy-start(f32[512]{0:T(512)} %param.25) | copy-start | bytes 6148
  93.8 8.3 %copy-start.5 = (f32[512]{0:T(512)S(1)}, f32[512]{0:T(512)}, u32[]{:S(2)}) copy-start(f32[512]{0:T(512)} %param.24) | copy-start | bytes 6148
  102.1 20.7 %copy-start.1 = (bf16[2048,512]{1,0:T(8,128)(2,1)S(1)}, bf16[2048,512]{1,0:T(8,128)(2,1)}, u32[]{:S(2)}) copy-start(bf16[2048,512]{1,0:T(8,128)(2,1)} %param.20) | copy-start | bytes 6291460
  102.1 20.7 %copy-start.6 = (f32[512]{0:T(512)S(1)}, f32[512]{0:T(512)}, u32[]{:S(2)}) copy-start(f32[512]{0:T(512)} %param.21) | copy-start | bytes 6148

commit v2 on v0

v2 whole, which is shorter than its diff:
```python
import jax
import jax.numpy as jnp
from jax import lax
from jax.experimental import pallas as pl
from jax.experimental.pallas import tpu as pltpu
from jax.sharding import PartitionSpec as P

LN_EPS = 1e-6
F32 = jnp.float32
BF16 = jnp.bfloat16
MESH = pl.DeviceIdType.MESH
PIECES = (
    ("xyz", "xyz"),
    ("yzx", "yxz"),
    ("zxy", "zyx"),
    ("xyz", "xzy"),
    ("yzx", "yxz"),
    ("zxy", "zyx"),
    ("xyz", "xyz"),
    ("yxz", "yxz"),
)
N = len(PIECES)
K = N // 2
STEP = 3
ROWS = 2
BLOCKS = 32 // ROWS
C0 = 0.7978845608028654
C1 = C0 * 0.044715


def layer_norm(values, ln_gain, ln_bias):
    mean_val = jnp.mean(values, axis=-1, keepdims=True)
    centred = values - mean_val
    var_val = jnp.mean(centred * centred, axis=-1, keepdims=True)
    return centred * lax.rsqrt(var_val + LN_EPS) * ln_gain + ln_bias


def gelu(a):
    half = 0.5 * a
    return half + half * jnp.tanh(a * (C0 + C1 * (a * a)))


def mixer_kernel(
    x_hbm, w1_ref, b1_ref, w2_ref, b2_ref, wc1_hbm, bc1_ref, wc2_hbm, bc2_ref, g1_ref, h1_ref, g2_ref, h2_ref, z_hbm,
    xv, w1o, w1t, w2t, b2c, wc1, wc2, tile_in, tile_all, usend, ustage, uall, relay, hb, rq, rd, rs, hq, rr, gall,
    send_sems, recv_sems, local_sems,
):
    me = lax.axis_index("sp")
    co = {"z": me // 32, "y": (me // 8) % 4, "x": (me // 2) % 4}
    core = me % 2
    other = 1 - core

    def device(c=None, **at):
        z, y, x = (at.get(a, co[a]) for a in "zyx")
        return ((z * 4 + y) * 4 + x) * 2 + (core if c is None else c)

    hop = {a: [co[a]] + [(co[a] + s) % 4 for s in (1, 2, 3)] for a in "xyz"}
    near = {a: [None] + [device(**{a: hop[a][s]}) for s in (1, 2, 3)] for a in "xyz"}
    partner = device(c=other)
    group = [device(c=(core + j) % 2, x=hop["x"][s]) for s in range(4) for j in range(2) if (s, j) != (0, 0)]
    sent = []

    def remote(src, dst, to):
        n = len(sent)
        copy = pltpu.make_async_remote_copy(
            src_ref=src, dst_ref=dst, send_sem=send_sems.at[n], recv_sem=recv_sems.at[n],
            device_id={"sp": to}, device_id_type=MESH,
        )
        sent.append(copy)
        return copy

    def start(copies):
        for copy in copies:
            copy.start()

    def arrive(copies):
        for copy in copies:
            copy.wait_recv()

    def local(src, dst, n):
        return pltpu.make_async_copy(src, dst, local_sems.at[n])

    loads = [local(x_hbm.at[pl.ds(8 * k, 8)], xv.at[pl.ds(8 * k, 8)], k) for k in range(K)]
    loads += [local(wc1_hbm, wc1, K), local(wc2_hbm, wc2, K + 1)]

    def lanes(pos, c):
        return pl.ds(pl.multiple_of((pos * 2 + c) * 128, 128), 128)

    w1_ring, w1_mine, w1_share = {}, {}, {}
    for i, a in enumerate("xyz"):
        dst = w1t.at[i, :, lanes(co[a], core)]
        w1_ring[a] = [remote(w1o, dst, near[a][s]) for s in (1, 2, 3)]
        w1_mine[a] = remote(w1o, dst, partner)
        refs = [w1t.at[i, :, lanes(hop[a][s], core)] for s in (3, 2, 1)]
        w1_share[a] = [remote(ref, ref, partner) for ref in refs]
    slot = co["x"] * 2 + core
    b1_group = [remote(tile_in.at[8], tile_in.at[slot], to) for to in group]
    ref = tile_all.at[co["z"], co["y"]]
    b1_y = [remote(ref, ref, near["y"][s]) for s in (1, 2, 3)]
    ref = tile_all.at[co["z"]]
    b1_z = [remote(ref, ref, near["z"][s]) for s in (1, 2, 3)]
    pairs = [remote(usend.at[k], ustage.at[k, :, core], partner) for k in range(K)]

    class Piece:
        pass

    pieces = []
    for j, (axes, order) in enumerate(PIECES):
        s = Piece()
        s.k, s.h, s.axes, s.order = j // 2, j % 2, axes, order
        a, b, c = axes
        low = s.h * 256
        s.half = half = (pl.ds(low, 128), pl.ds(low + 128, 128))
        s.lanes = pl.ds(low, 256)
        s.at = (co[a], co[c], co[b])
        p, st = hop[a], ustage.at[s.k]
        s.passing = [
            remote(st.at[p[2], :, :, half[0]], relay.at[j, 0], near[a][1]),
            remote(st.at[p[2], :, :, half[1]], relay.at[j, 1], near[a][3]),
        ]
        s.direct = [
            remote(st.at[p[1], :, :, s.lanes], uall.at[j, p[0]], near[a][1]),
            remote(st.at[p[3], :, :, s.lanes], uall.at[j, p[0]], near[a][3]),
        ]
        s.forward = [
            remote(relay.at[j, 0], uall.at[j, p[3], :, :, pl.ds(0, 128)], near[a][1]),
            remote(relay.at[j, 1], uall.at[j, p[1], :, :, pl.ds(128, 128)], near[a][3]),
        ]
        q = hop[b]
        s.part = lambda pos, i, j=j: hb.at[j, :, pos, :, pl.ds(128 * i, 128)]
        s.first = [remote(s.part(q[2], 0), rq.at[j, 0], near[b][1]), remote(s.part(q[2], 1), rq.at[j, 1], near[b][3])]
        s.straight = [remote(s.part(q[1], 1), rd.at[j, 0], near[b][1]), remote(s.part(q[3], 0), rd.at[j, 1], near[b][3])]
        s.second = [remote(s.part(q[1], 0), rs.at[j, 0], near[b][1]), remote(s.part(q[3], 1), rs.at[j, 1], near[b][3])]
        s.last = [remote(hq.at[j, hop[c][d]], rr.at[j, d], near[c][d]) for d in (1, 3, 2)]

        def block(known, axis=None, pos=None, lane=None, s=s):
            names = (s.axes[0], s.axes[2], s.axes[1])
            at = tuple(pos if n == axis else slice(None) if n in known else v for n, v in zip(names, s.at))
            return gall.at[(s.k, core) + at + (slice(None), s.lanes if lane is None else s.half[lane])]

        d0, d1, d2 = order
        own = block("")
        s.gather0 = [remote(own, own, near[d0][d]) for d in (1, 3, 2)]
        own = block(d0)
        s.gather1 = [remote(own, own, near[d1][d]) for d in (1, 3, 2)]
        own = block(d0 + d1)
        s.gather2 = [remote(own, own, near[d2][1]), remote(own, own, near[d2][3])]
        ends = [block(d0 + d1, d2, hop[d2][3], 0), block(d0 + d1, d2, hop[d2][1], 1)]
        s.gather3 = [remote(ends[0], ends[0], near[d2][1]), remote(ends[1], ends[1], near[d2][3])]
        whole = gall.at[s.k, core, :, :, :, :, s.lanes]
        s.share = remote(whole, whole, partner)
        pieces.append(s)

    gain1, bias1 = g1_ref[...], h1_ref[...]

    def norm(k):
        loads[k].wait()

        def body(i, carry):
            mine = layer_norm(xv[8 * k + 4 * core + i].astype(F32), gain1, bias1).astype(BF16)
            ustage[k, i, core] = mine
            theirs = layer_norm(xv[8 * k + 4 * other + i].astype(F32), gain1, bias1).astype(BF16)
            usend[k, i] = theirs
            return carry

        lax.fori_loop(0, 4, body, 0)
        pairs[k].start()

    def exchange(j, s):
        if s.h == 0:
            pairs[s.k].wait_recv()
        start(s.passing)
        start(s.direct)
        uall[j, s.at[0]] = ustage[s.k, s.at[0], :, :, s.lanes]

    def pass_on(j, s):
        for came, go in zip(s.passing, s.forward):
            came.wait_recv()
            go.start()

    def mix(j, s):
        arrive(s.direct + s.forward)
        u = uall[j].reshape(1024, 256)
        part = jnp.dot(w1t["xyz".index(s.axes[0])], u, preferred_element_type=F32)
        hb[j] = part.reshape(4, 4, 16, 256)
        start(s.first + s.straight)

    def sum_q(j, s):
        q = hop[s.axes[1]]
        for i, pos in enumerate((q[1], q[3])):
            s.first[i].wait_recv()
            ref = s.part(pos, i)
            ref[...] = ref[...] + rq[j, i]
            s.second[i].start()

    def start_r(j, s):
        arrive(s.straight + s.second)
        q = co[s.axes[1]]
        hq[j, :, :, pl.ds(0, 128)] = s.part(q, 0)[...] + rd[j, 1] + rs[j, 0]
        hq[j, :, :, pl.ds(128, 128)] = s.part(q, 1)[...] + rd[j, 0] + rs[j, 1]
        start(s.last)

    def activate(j, s):
        arrive(s.last)
        a, b, c = s.axes
        tile = tile_all[co[c], co[b]]
        total = hq[j, co[c]] + rr[j, 1] + rr[j, 2] + rr[j, 3] + jnp.concatenate([tile, tile], axis=1)
        gall[s.k, core, s.at[0], s.at[1], s.at[2], :, s.lanes] = gelu(total).astype(BF16)
        start(s.gather0)

    def gather1(j, s):
        arrive(s.gather0)
        start(s.gather1)

    def gather2(j, s):
        arrive(s.gather1)
        start(s.gather2)

    def gather3(j, s):
        for came, go in zip(s.gather2, s.gather3):
            came.wait_recv()
            go.start()

    def share(j, s):
        arrive(s.gather3)
        s.share.start()

    def finish(j, s):
        s.share.wait_recv()

    STEPS = (exchange, pass_on, mix, sum_q, start_r, activate, gather1, gather2, gather3, share, finish)

    def channel_mix(i):
        gain2, bias2 = g2_ref[...], h2_ref[...]
        shift = b2c[...]
        shift = jnp.concatenate([shift] * 4, axis=1)
        mids = []
        for n in range(ROWS):
            img = i * ROWS + n
            act = gall[img // 8, (img // 4) % 2, img % 4].reshape(256, 512)
            tok = jnp.dot(w2t[...], act, preferred_element_type=F32) + shift
            mids.append((xv[img].astype(F32) + tok).astype(BF16).astype(F32))
        mid = jnp.concatenate(mids, axis=0)
        v = layer_norm(mid, gain2, bias2).astype(BF16)
        total = mid + bc2_ref[...]
        for f in range(0, 2048, 512):
            pre = jnp.dot(v, wc1[:, f:f + 512], preferred_element_type=F32) + bc1_ref[:, f:f + 512]
            total = total + jnp.dot(gelu(pre).astype(BF16), wc2[f:f + 512, :], preferred_element_type=F32)
        xv[pl.ds(i * ROWS, ROWS)] = total.astype(BF16).reshape(ROWS, 128, 512)

    def store(i):
        window = pl.ds(i * ROWS, ROWS)
        return local(xv.at[window], z_hbm.at[window], K + 2)

    start(loads)
    barrier = pltpu.get_barrier_semaphore()
    peers = group + [near[a][s] for a in "yz" for s in (1, 2, 3)]
    for peer in peers:
        pl.semaphore_signal(barrier, inc=1, device_id={"sp": peer}, device_id_type=MESH)
    w1o[...] = w1_ref[...].T
    w2t[...] = w2_ref[...].T
    b2c[...] = jnp.broadcast_to(b2_ref[...], (128, 128)).T
    row = lax.broadcasted_iota(jnp.int32, (16, 128), 0)
    tile_in[8] = jnp.where(row == 2 * slot, b1_ref[0], jnp.where(row == 2 * slot + 1, b1_ref[1], 0.0))
    tile_in[slot] = tile_in[8]
    for i, a in enumerate("xyz"):
        w1t[i, :, lanes(co[a], core)] = w1o[...]
    pl.semaphore_wait(barrier, len(peers))

    norm(0)
    for a in "xyz":
        start(w1_ring[a])
    start([w1_mine[a] for a in "xyz"])
    start(b1_group)
    norm(1)
    for j in (0, 1):
        exchange(j, pieces[j])
    norm(2)
    for j in (2, 3):
        exchange(j, pieces[j])
    norm(3)

    arrive(b1_group)
    tile = tile_in[0]
    for n in range(1, 8):
        tile = tile + tile_in[n]
    tile_all[co["z"], co["y"]] = tile
    start(b1_y)
    for a in "xyz":
        for came, go in zip(w1_ring[a], w1_share[a]):
            came.wait_recv()
            go.start()
    for j in (0, 1):
        pass_on(j, pieces[j])
    arrive(b1_y)
    start(b1_z)
    for a in "xyz":
        arrive([w1_mine[a]] + w1_share[a])
    arrive(b1_z)

    ticks = {}
    for k in range(K):
        for n in range(len(STEPS)):
            ticks.setdefault(n + STEP * k, []).append((n, k))
    first_block = len(STEPS) - 1
    slots = {}
    for t in sorted(ticks):
        todo = [(n, k) for n, k in sorted(ticks[t], key=lambda nk: -nk[0]) if not (n == 0 and k < 2 or n == 1 and k < 1)]

        def run(todo=todo):
            for n, k in todo:
                for j in (2 * k, 2 * k + 1):
                    STEPS[n](j, pieces[j])

        if t <= first_block:
            run()
        else:
            slots.setdefault(((t - first_block) * (8 // ROWS)) // STEP, []).append(run)

    def loop(i, carry):
        for s, runs in slots.items():
            @pl.when(i == s)
            def _():
                for run in runs:
                    run()
        channel_mix(i)
        store(i).start()
        return carry

    loads[K].wait()
    loads[K + 1].wait()
    lax.fori_loop(0, BLOCKS, loop, 0)
    local(xv, z_hbm, K + 2).wait()
    for copy in sent:
        copy.wait_send()


N_COPIES = 27 * N + K + 3 * 7 + 7 + 3 + 3


def vmem(*shape, dtype=BF16):
    return pltpu.VMEM(shape, dtype)


def mixer(x, w1, b1, w2, b2, wc1, bc1, wc2, bc2, g1, h1, g2, h2):
    any_space = pl.BlockSpec(memory_space=pl.ANY)
    whole = pl.BlockSpec(memory_space=pltpu.VMEM)
    scalars = pl.BlockSpec(memory_space=pltpu.SMEM)
    return pl.pallas_call(
        mixer_kernel,
        name="mixer",
        out_shape=jax.ShapeDtypeStruct((32, 128, 512), BF16),
        in_specs=[any_space, whole, scalars, whole, whole, any_space, whole, any_space, whole, whole, whole, whole, whole],
        out_specs=any_space,
        scratch_shapes=[
            vmem(32, 128, 512),
            vmem(256, 128),
            vmem(3, 256, 1024),
            vmem(128, 256),
            vmem(128, 128, dtype=F32),
            vmem(512, 2048),
            vmem(2048, 512),
            vmem(9, 16, 128, dtype=F32),
            vmem(4, 4, 16, 128, dtype=F32),
            vmem(K, 4, 128, 512),
            vmem(K, 4, 2, 128, 512),
            vmem(N, 4, 2, 128, 256),
            vmem(N, 2, 2, 128, 128),
            vmem(N, 4, 4, 16, 256, dtype=F32),
            vmem(N, 2, 4, 16, 128, dtype=F32),
            vmem(N, 2, 4, 16, 128, dtype=F32),
            vmem(N, 2, 4, 16, 128, dtype=F32),
            vmem(N, 4, 16, 256, dtype=F32),
            vmem(N, 4, 16, 256, dtype=F32),
            vmem(K, 2, 4, 4, 4, 16, 512),
            pltpu.SemaphoreType.DMA((N_COPIES,)),
            pltpu.SemaphoreType.DMA((N_COPIES,)),
            pltpu.SemaphoreType.DMA((K + 3,)),
        ],
        compiler_params=pltpu.CompilerParams(
            collective_id=0, has_side_effects=True, vmem_limit_bytes=60 * 1024 * 1024
        ),
    )(
        x, w1, b1, w2, b2.reshape(1, 128), wc1, bc1.reshape(1, 2048), wc2, bc2.reshape(1, 512),
        g1.reshape(1, 512), h1.reshape(1, 512), g2.reshape(1, 512), h2.reshape(1, 512),
    )


def solution(mesh):
    row_spec = P("dp", "sp", None)
    in_specs = (row_spec, P("sp", None), P("sp"), P(None, "sp"), P("sp"), P(None, None), P(None), P(None, None), P(None), P(None), P(None), P(None), P(None))
    return jax.shard_map(mixer, mesh=mesh, in_specs=in_specs, out_specs=row_spec, check_vma=False)
```

time: 855 us -> 129 us (0.15)
  waiting for transfers between devices: 740 us -> 0 us
  Pallas kernels: 0 us -> 122 us
  matrix products: 56.9 us -> 0 us
  local copies, waits for them, and re-layouts: 33.2 us -> 4.64 us
  between operations: 13.6 us -> 0.01 us
  other arithmetic: 9.62 us -> 0 us
    reduce_scatter x1 -> x0, waiting for transfers between devices: 668 us -> none  [local_layer(): lax.psum_scatter(part_pre, 'sp', scatter_dimension=1, tiled=True)]
    pallas_call x0 -> x1, Pallas kernels: none -> 122 us  [mixer(): pl.pallas_call(mixer_kernel, name='mixer', out_shape=jax.ShapeDtypeStruct...]
    all_gather x1 -> x0, waiting for transfers between devices: 71.8 us -> none  [local_layer(): act_full = lax.all_gather(tok_act, 'sp', axis=1, tiled=True)]
    dot_general x4 -> x0, matrix products: 56.9 us -> none  [the longest x1 20.6 us: channel_mix(): jnp.einsum('bsc,cf->bsf', normed_two, w_ch1, preferred_element_type=jnp.f...]
    transpose x1 -> x0, local copies, waits for them, and re-layouts: 20.2 us -> none  [local_layer(): jnp.einsum('bsc,sd->bdc', normed, w1_rows, preferred_element_type=jnp.flo...]
  transfers between devices with their start and end apart: 2 -> 0, of which waited for: 2 -> 0; matrix products, arithmetic and copies ran while one was open for 0% -> 0% of each run, Pallas kernels for 0% -> 0%
where the time goes in v2:
time: 129 us; the launch traced here: 126 us
  Pallas kernels  122 us (95%)
  local copies, waits for them, and re-layouts  4.64 us (4%)
    pallas_call x1, Pallas kernels, mixer(): pl.pallas_call(mixer_kernel, name='mixer', out_shape=jax.ShapeDtypeStruct...  122 us
    unnamed x1, local copies, waits for them, and re-layouts  4.64 us

profile of v2, /device:TPU:1, one launch (start us, length us, event | category | flops | bytes accessed | tf_op | source)
XLA Modules:
  0.0 126.2 jit_solution(4238085423238465574)
XLA Ops:
  0.0 121.6 %mixer.1 = bf16[32,128,512]{2,1,0:T(8,128)(2,1)} custom-call(bf16[32,128,512]{2,1,0:T(8,128)(2,1)} %x_hbm.1, bf16[128,256]{1,0:T(8,128)(2,1)} %w1_ref.1, f32[2]{0:T(128)} %b1_ref.1, bf16[256,128]{1,0:T(8,128)(2,1)} %w2_ref.1, f32[1,128]{1,0:T(1,128)} %bitcast.13, bf16[512,2048]{1,0:T(8,128)(2,1)} %wc1_hbm.1, f32[1,2048]{1,0:T(1,128)} %bitcast.7, ...), custom_call_target="tpu_custom_call" | custom-call | tf_op jit(solution)/shard_map/mixer/pallas_call | solution.py:349
  121.6 4.6 %copy.15 = bf16[32,128,512]{2,1,0:T(8,128)(2,1)} copy(bf16[32,128,512]{2,1,0:T(8,128)(2,1)} %mixer.1) | data formatting | bytes 8388608

commit v3 on v2

--- a/solution.py
+++ b/solution.py
@@ -10,18 +10,29 @@
 BF16 = jnp.bfloat16
 MESH = pl.DeviceIdType.MESH
 PIECES = (
+    ("xyz", "zyx"),
+    ("zxy", "xyz"),
+    ("yxz", "xzy"),
+    ("zxy", "zyx"),
+    ("yxz", "zxy"),
     ("xyz", "xyz"),
-    ("yzx", "yxz"),
     ("zxy", "zyx"),
-    ("xyz", "xzy"),
-    ("yzx", "yxz"),
-    ("zxy", "zyx"),
-    ("xyz", "xyz"),
-    ("yxz", "yxz"),
+    ("yxz", "xzy"),
 )
 N = len(PIECES)
 K = N // 2
-STEP = 3
+NORM, W1_PASS, MLP = 11, 12, 15
+ORDER = (
+    (11, 1), (11, 2), (0, 0), (0, 1), (11, 3), (0, 2), (1, 2), (12, 0), (1, 1), (0, 3), (0, 4), (1, 0), (0, 5),
+    (13, 0), (2, 0), (2, 1), (2, 2), (1, 3), (1, 4), (1, 5), (0, 6), (3, 0), (0, 7), (3, 1), (14, 0), (3, 2),
+    (2, 3), (2, 4), (4, 0), (1, 6), (2, 5), (4, 1), (1, 7), (4, 2), (3, 3), (3, 4), (5, 0), (3, 5), (2, 6), (4, 3),
+    (5, 2), (5, 1), (4, 4), (2, 7), (6, 0), (4, 5), (3, 6), (5, 3), (6, 2), (6, 1), (5, 4), (3, 7), (5, 5), (4, 6),
+    (7, 0), (6, 3), (4, 7), (7, 2), (7, 1), (6, 4), (6, 5), (5, 6), (8, 0), (7, 3), (5, 7), (7, 4), (8, 2), (8, 1),
+    (6, 6), (9, 0), (7, 5), (10, 0), (9, 1), (8, 3), (8, 4), (6, 7), (10, 1), (15, 0), (9, 2), (15, 1), (10, 2),
+    (9, 3), (8, 5), (15, 2), (10, 3), (9, 4), (7, 6), (7, 7), (15, 3), (10, 4), (15, 4), (9, 5), (15, 5), (10, 5),
+    (15, 6), (8, 6), (8, 7), (15, 7), (15, 8), (15, 9), (9, 6), (9, 7), (15, 10), (10, 6), (10, 7), (15, 11),
+    (15, 12), (15, 13), (15, 14), (15, 15),
+)
 ROWS = 2
 BLOCKS = 32 // ROWS
 C0 = 0.7978845608028654
@@ -42,7 +53,7 @@
 
 def mixer_kernel(
     x_hbm, w1_ref, b1_ref, w2_ref, b2_ref, wc1_hbm, bc1_ref, wc2_hbm, bc2_ref, g1_ref, h1_ref, g2_ref, h2_ref, z_hbm,
-    xv, w1o, w1t, w2t, b2c, wc1, wc2, tile_in, tile_all, usend, ustage, uall, relay, hb, rq, rd, rs, hq, rr, gall,
+    xv, w1o, w1t, w2t, b2c, wc1, wc2, tile_in, tile_all, usend, ustage, uall, relay, hb, rq, rd, rs, hq, rr, gall, v0, v1, mid0, mid1,
     send_sems, recv_sems, local_sems,
 ):
     me = lax.axis_index("sp")
@@ -147,8 +158,10 @@
         s.gather2 = [remote(own, own, near[d2][1]), remote(own, own, near[d2][3])]
         ends = [block(d0 + d1, d2, hop[d2][3], 0), block(d0 + d1, d2, hop[d2][1], 1)]
         s.gather3 = [remote(ends[0], ends[0], near[d2][1]), remote(ends[1], ends[1], near[d2][3])]
-        whole = gall.at[s.k, core, :, :, :, :, s.lanes]
-        s.share = remote(whole, whole, partner)
+        s.share = []
+        for d in (0, 1, 3, 2):
+            ref = block(d0 + d1, d2, hop[d2][d], None)
+            s.share.append(remote(ref, ref, partner))
         pieces.append(s)
 
     gain1, bias1 = g1_ref[...], h1_ref[...]
@@ -164,7 +177,6 @@
             return carry
 
         lax.fori_loop(0, 4, body, 0)
-        pairs[k].start()
 
     def exchange(j, s):
         if s.h == 0:
@@ -215,36 +227,37 @@
     def gather2(j, s):
         arrive(s.gather1)
         start(s.gather2)
+        s.share[0].start()
 
     def gather3(j, s):
-        for came, go in zip(s.gather2, s.gather3):
+        for i, (came, go) in enumerate(zip(s.gather2, s.gather3)):
             came.wait_recv()
             go.start()
+        start(s.share[1:3])
 
     def share(j, s):
         arrive(s.gather3)
-        s.share.start()
+        s.share[3].start()
 
     def finish(j, s):
-        s.share.wait_recv()
+        arrive(s.share)
 
     STEPS = (exchange, pass_on, mix, sum_q, start_r, activate, gather1, gather2, gather3, share, finish)
 
-    def channel_mix(i):
-        gain2, bias2 = g2_ref[...], h2_ref[...]
-        shift = b2c[...]
-        shift = jnp.concatenate([shift] * 4, axis=1)
-        mids = []
+    def token_half(i, v_ref, mid_ref):
+        shift = jnp.concatenate([b2c[...]] * 4, axis=1)
         for n in range(ROWS):
             img = i * ROWS + n
             act = gall[img // 8, (img // 4) % 2, img % 4].reshape(256, 512)
             tok = jnp.dot(w2t[...], act, preferred_element_type=F32) + shift
-            mids.append((xv[img].astype(F32) + tok).astype(BF16).astype(F32))
-        mid = jnp.concatenate(mids, axis=0)
-        v = layer_norm(mid, gain2, bias2).astype(BF16)
-        total = mid + bc2_ref[...]
+            mid = (xv[img].astype(F32) + tok).astype(BF16)
+            mid_ref[128 * n:128 * n + 128, :] = mid
+            v_ref[128 * n:128 * n + 128, :] = layer_norm(mid.astype(F32), g2_ref[...], h2_ref[...]).astype(BF16)
+
+    def channel_half(i, v_ref, mid_ref):
+        total = mid_ref[...].astype(F32) + bc2_ref[...]
         for f in range(0, 2048, 512):
-            pre = jnp.dot(v, wc1[:, f:f + 512], preferred_element_type=F32) + bc1_ref[:, f:f + 512]
+            pre = jnp.dot(v_ref[...], wc1[:, f:f + 512], preferred_element_type=F32) + bc1_ref[:, f:f + 512]
             total = total + jnp.dot(gelu(pre).astype(BF16), wc2[f:f + 512, :], preferred_element_type=F32)
         xv[pl.ds(i * ROWS, ROWS)] = total.astype(BF16).reshape(ROWS, 128, 512)
 
@@ -258,84 +271,88 @@
     for peer in peers:
         pl.semaphore_signal(barrier, inc=1, device_id={"sp": peer}, device_id_type=MESH)
     w1o[...] = w1_ref[...].T
-    w2t[...] = w2_ref[...].T
-    b2c[...] = jnp.broadcast_to(b2_ref[...], (128, 128)).T
+    norm(0)
+    pl.semaphore_wait(barrier, len(peers))
+    pairs[0].start()
+    for a in "xyz":
+        start(w1_ring[a])
     row = lax.broadcasted_iota(jnp.int32, (16, 128), 0)
     tile_in[8] = jnp.where(row == 2 * slot, b1_ref[0], jnp.where(row == 2 * slot + 1, b1_ref[1], 0.0))
     tile_in[slot] = tile_in[8]
+    start(b1_group)
+    start([w1_mine[a] for a in "xyz"])
     for i, a in enumerate("xyz"):
         w1t[i, :, lanes(co[a], core)] = w1o[...]
-    pl.semaphore_wait(barrier, len(peers))
-
-    norm(0)
-    for a in "xyz":
-        start(w1_ring[a])
-    start([w1_mine[a] for a in "xyz"])
-    start(b1_group)
-    norm(1)
-    for j in (0, 1):
-        exchange(j, pieces[j])
-    norm(2)
-    for j in (2, 3):
-        exchange(j, pieces[j])
-    norm(3)
-
-    arrive(b1_group)
-    tile = tile_in[0]
-    for n in range(1, 8):
-        tile = tile + tile_in[n]
-    tile_all[co["z"], co["y"]] = tile
-    start(b1_y)
-    for a in "xyz":
-        for came, go in zip(w1_ring[a], w1_share[a]):
-            came.wait_recv()
-            go.start()
-    for j in (0, 1):
-        pass_on(j, pieces[j])
-    arrive(b1_y)
-    start(b1_z)
-    for a in "xyz":
-        arrive([w1_mine[a]] + w1_share[a])
-    arrive(b1_z)
-
-    ticks = {}
-    for k in range(K):
-        for n in range(len(STEPS)):
-            ticks.setdefault(n + STEP * k, []).append((n, k))
-    first_block = len(STEPS) - 1
-    slots = {}
-    for t in sorted(ticks):
-        todo = [(n, k) for n, k in sorted(ticks[t], key=lambda nk: -nk[0]) if not (n == 0 and k < 2 or n == 1 and k < 1)]
-
-        def run(todo=todo):
-            for n, k in todo:
-                for j in (2 * k, 2 * k + 1):
-                    STEPS[n](j, pieces[j])
-
-        if t <= first_block:
-            run()
+    w2t[...] = w2_ref[...].T
+    b2c[...] = jnp.broadcast_to(b2_ref[...], (128, 128)).T
+
+    def later_norm(k):
+        norm(k)
+        pairs[k].start()
+
+    def w1_pass():
+        for a in "xyz":
+            for came, go in zip(w1_ring[a], w1_share[a]):
+                came.wait_recv()
+                go.start()
+        arrive(b1_group)
+        tile = tile_in[0]
+        for n in range(1, 8):
+            tile = tile + tile_in[n]
+        tile_all[co["z"], co["y"]] = tile
+        start(b1_y)
+
+    def w1_end():
+        for a in "xyz":
+            arrive([w1_mine[a]] + w1_share[a])
+        arrive(b1_y)
+        start(b1_z)
+
+    def b1_end():
+        arrive(b1_z)
+
+    def run(op):
+        n, j = op
+        if n < len(STEPS):
+            STEPS[n](j, pieces[j])
+        elif n == NORM:
+            later_norm(j)
         else:
-            slots.setdefault(((t - first_block) * (8 // ROWS)) // STEP, []).append(run)
-
-    def loop(i, carry):
-        for s, runs in slots.items():
-            @pl.when(i == s)
-            def _():
-                for run in runs:
-                    run()
-        channel_mix(i)
-        store(i).start()
-        return carry
-
+            (w1_pass, w1_end, b1_end)[n - W1_PASS]()
+
+    slots, slot_no = {}, 0
+    for op in ORDER:
+        if op[0] == MLP:
+            slot_no = op[1] + 1
+        else:
+            slots.setdefault(slot_no, []).append(op)
+    for op in slots.pop(0, []):
+        run(op)
     loads[K].wait()
     loads[K + 1].wait()
-    lax.fori_loop(0, BLOCKS, loop, 0)
+    token_half(0, v0, mid0)
+
+    def loop(p, carry):
+        for side, (mine, ahead) in enumerate((((v0, mid0), (v1, mid1)), ((v1, mid1), (v0, mid0)))):
+            i = 2 * p + side
+            for s, ops in slots.items():
+                if s % 2 == side:
+                    @pl.when(p == s // 2)
+                    def _():
+                        for op in ops:
+                            run(op)
+            token_half(jnp.minimum(i + 1, BLOCKS - 1), *ahead)
+            channel_half(i, *mine)
+            store(i).start()
+        return carry
+
+    lax.fori_loop(0, BLOCKS // 2, loop, 0)
     local(xv, z_hbm, K + 2).wait()
     for copy in sent:
         copy.wait_send()
 
 
-N_COPIES = 27 * N + K + 3 * 7 + 7 + 3 + 3
+N_COPIES = 30 * N + K + 3 * 7 + 7 + 3 + 3
 
 
 def vmem(*shape, dtype=BF16):
@@ -373,6 +390,10 @@
             vmem(N, 4, 16, 256, dtype=F32),
             vmem(N, 4, 16, 256, dtype=F32),
             vmem(K, 2, 4, 4, 4, 16, 512),
+            vmem(128 * ROWS, 512),
+            vmem(128 * ROWS, 512),
+            vmem(128 * ROWS, 512),
+            vmem(128 * ROWS, 512),
             pltpu.SemaphoreType.DMA((N_COPIES,)),
             pltpu.SemaphoreType.DMA((N_COPIES,)),
             pltpu.SemaphoreType.DMA((K + 3,)),

time: 129 us -> 102 us (0.79); the launches traced: 126 us -> 102 us
  Pallas kernels: 122 us -> 97 us
    pallas_call x1, Pallas kernels: 122 us -> 97 us  [mixer(): pl.pallas_call(mixer_kernel, name='mixer', out_shape=jax.ShapeDtypeStruct...]
where the time goes in v3:
time: 102 us
  Pallas kernels  97 us (95%)
  local copies, waits for them, and re-layouts  4.64 us (5%)
    pallas_call x1, Pallas kernels, mixer(): pl.pallas_call(mixer_kernel, name='mixer', out_shape=jax.ShapeDtypeStruct...  97 us
    unnamed x1, local copies, waits for them, and re-layouts  4.64 us

profile of v3, /device:TPU:1, one launch (start us, length us, event | category | flops | bytes accessed | tf_op | source)
XLA Modules:
  0.0 101.6 jit_solution(4287674338314220258)
XLA Ops:
  0.0 97.0 %mixer.1 = bf16[32,128,512]{2,1,0:T(8,128)(2,1)} custom-call(bf16[32,128,512]{2,1,0:T(8,128)(2,1)} %x_hbm.1, bf16[128,256]{1,0:T(8,128)(2,1)} %w1_ref.1, f32[2]{0:T(128)} %b1_ref.1, bf16[256,128]{1,0:T(8,128)(2,1)} %w2_ref.1, f32[1,128]{1,0:T(1,128)} %bitcast.13, bf16[512,2048]{1,0:T(8,128)(2,1)} %wc1_hbm.1, f32[1,2048]{1,0:T(1,128)} %bitcast.7, ...), custom_call_target="tpu_custom_call" | custom-call | tf_op jit(solution)/shard_map/mixer/pallas_call | solution.py:366
  97.0 4.6 %copy.15 = bf16[32,128,512]{2,1,0:T(8,128)(2,1)} copy(bf16[32,128,512]{2,1,0:T(8,128)(2,1)} %mixer.1) | data formatting | bytes 8388608

commit v4 on v3

v4 whole, which is shorter than its diff:
```python
import jax
import jax.numpy as jnp
from jax import lax
from jax.experimental import pallas as pl
from jax.experimental.pallas import tpu as pltpu
from jax.sharding import PartitionSpec as P

LN_EPS = 1e-6
F32 = jnp.float32
BF16 = jnp.bfloat16
MESH = pl.DeviceIdType.MESH
PIECES = (
    ("zyx", "xyz"),
    ("yzx", "xzy"),
    ("zxy", "zyx"),
    ("xyz", "zxy"),
    ("yzx", "yxz"),
    ("xzy", "yxz"),
    ("xzy", "zxy"),
    ("yxz", "xzy"),
)
N = len(PIECES)
NORM, W1_PASS = 11, 12
ORDER = (
    (111, 112, 0, 113, 114, 115, 1, 2, 116, 3, 117, 5, 11, 120, 10, 13, 4, 12, 130, 21, 15, 14, 6, 20, 23, 22, 24,
     25, 140, 30, 16, 7, 31, 33, 34, 40, 35, 32, 17, 41, 44, 26, 45, 50, 42, 43, 51, 36, 27, 54, 60, 55, 52, 53,
     61, 46, 37, 64, 70, 62, 63, 65, 47, 56, 71, 74, 72, 73, 80, 57, 66, 75, 81, 84, 82, 83, 90, 67, 91, 100,),
    (101, 76,),
    (92, 93, 85,),
    (102, 103, 94,),
    (104, 77,),
    (95, 86,),
    (105,),
    (),
    (87,),
    (96,),
    (106,),
    (97,),
    (107,),
    (),
    (),
    (),
)
BLOCKS = 2 * N
C0 = 0.7978845608028654
C1 = C0 * 0.044715


def layer_norm(values, ln_gain, ln_bias):
    mean_val = jnp.mean(values, axis=-1, keepdims=True)
    centred = values - mean_val
    var_val = jnp.mean(centred * centred, axis=-1, keepdims=True)
    return centred * lax.rsqrt(var_val + LN_EPS) * ln_gain + ln_bias


def gelu_of_half(h):
    return h + h * jnp.tanh(h * (2.0 * C0 + (8.0 * C1) * (h * h)))


def mixer_kernel(
    x_hbm, w1_hbm, b1_ref, w2_hbm, vec_hbm, wc1_hbm, bc1_hbm, wc2_hbm, z_hbm,
    xv, w1v, w2v, vec, bc1, w1o, w1t, w2t, b2c, wc1, wc2, tile_in, tile_all, usend, ustage, uall, relay,
    hb, rq, rd, rs, hq, rr, gall, va, vb, mida, midb, prea, preb, acta, actb, acc,
    send_sems, recv_sems, local_sems,
):
    me = lax.axis_index("sp")
    co = {"z": me // 32, "y": (me // 8) % 4, "x": (me // 2) % 4}
    core = me % 2
    other = 1 - core

    def device(c=None, **at):
        z, y, x = (at.get(a, co[a]) for a in "zyx")
        return ((z * 4 + y) * 4 + x) * 2 + (core if c is None else c)

    hop = {a: [co[a]] + [(co[a] + s) % 4 for s in (1, 2, 3)] for a in "xyz"}
    near = {a: [None] + [device(**{a: hop[a][s]}) for s in (1, 2, 3)] for a in "xyz"}
    partner = device(c=other)
    group = [device(c=(core + j) % 2, x=hop["x"][s]) for s in range(4) for j in range(2) if (s, j) != (0, 0)]
    sent = []

    def remote(src, dst, to):
        n = len(sent)
        copy = pltpu.make_async_remote_copy(
            src_ref=src, dst_ref=dst, send_sem=send_sems.at[n], recv_sem=recv_sems.at[n],
            device_id={"sp": to}, device_id_type=MESH,
        )
        sent.append(copy)
        return copy

    def start(copies):
        for copy in copies:
            copy.start()

    def arrive(copies):
        for copy in copies:
            copy.wait_recv()

    def local(src, dst, n):
        return pltpu.make_async_copy(src, dst, local_sems.at[n])

    loads = [local(x_hbm.at[pl.ds(4 * j, 4)], xv.at[pl.ds(4 * j, 4)], j) for j in range(N)]
    small = [local(vec_hbm, vec, N), local(w1_hbm, w1v, N + 1), local(w2_hbm, w2v, N + 2), local(bc1_hbm, bc1, N + 3)]
    large = [local(wc1_hbm, wc1, N + 4), local(wc2_hbm, wc2, N + 5)]

    def lanes(pos, c):
        return pl.ds(pl.multiple_of((pos * 2 + c) * 128, 128), 128)

    rings = sorted({axes[0] for axes, _ in PIECES})
    w1_ring, w1_mine, w1_share = {}, {}, {}
    for i, a in enumerate(rings):
        dst = w1t.at[i, :, lanes(co[a], core)]
        w1_ring[a] = [remote(w1o, dst, near[a][s]) for s in (1, 2, 3)]
        w1_mine[a] = remote(w1o, dst, partner)
        refs = [w1t.at[i, :, lanes(hop[a][s], core)] for s in (3, 2, 1)]
        w1_share[a] = [remote(ref, ref, partner) for ref in refs]
    slot = co["x"] * 2 + core
    b1_group = [remote(tile_in.at[8], tile_in.at[slot], to) for to in group]
    ref = tile_all.at[co["z"], co["y"]]
    b1_y = [remote(ref, ref, near["y"][s]) for s in (1, 2, 3)]
    ref = tile_all.at[co["z"]]
    b1_z = [remote(ref, ref, near["z"][s]) for s in (1, 2, 3)]

    class Piece:
        pass

    low, high = pl.ds(0, 128), pl.ds(128, 128)
    half = (low, high)
    pieces = []
    for j, (axes, order) in enumerate(PIECES):
        s = Piece()
        s.axes = axes
        a, b, c = axes
        s.at = (co[a], co[c], co[b])
        s.pair = remote(usend.at[j], ustage.at[j, :, core], partner)
        p, st = hop[a], ustage.at[j]
        s.passing = [
            remote(st.at[p[2], :, :, low], relay.at[j, 0], near[a][1]),
            remote(st.at[p[2], :, :, high], relay.at[j, 1], near[a][3]),
        ]
        s.direct = [
            remote(st.at[p[1]], uall.at[j, p[0]], near[a][1]),
            remote(st.at[p[3]], uall.at[j, p[0]], near[a][3]),
        ]
        s.forward = [
            remote(relay.at[j, 0], uall.at[j, p[3], :, :, low], near[a][1]),
            remote(relay.at[j, 1], uall.at[j, p[1], :, :, high], near[a][3]),
        ]
        q = hop[b]
        s.part = lambda pos, i, j=j: hb.at[j, :, pos, :, half[i]]
        s.first = [remote(s.part(q[2], 0), rq.at[j, 0], near[b][1]), remote(s.part(q[2], 1), rq.at[j, 1], near[b][3])]
        s.straight = [remote(s.part(q[1], 1), rd.at[j, 0], near[b][1]), remote(s.part(q[3], 0), rd.at[j, 1], near[b][3])]
        s.second = [remote(s.part(q[1], 0), rs.at[j, 0], near[b][1]), remote(s.part(q[3], 1), rs.at[j, 1], near[b][3])]
        s.last = [remote(hq.at[j, hop[c][d]], rr.at[j, d], near[c][d]) for d in (1, 3, 2)]

        def block(known, axis=None, pos=None, lane=slice(None), s=s, j=j):
            names = (s.axes[0], s.axes[2], s.axes[1])
            at = tuple(pos if n == axis else slice(None) if n in known else v for n, v in zip(names, s.at))
            return gall.at[(j, core) + at + (slice(None), lane)]

        d0, d1, d2 = order
        own = block("")
        s.gather0 = [remote(own, own, near[d0][d]) for d in (1, 3, 2)]
        own = block(d0)
        s.gather1 = [remote(own, own, near[d1][d]) for d in (1, 3, 2)]
        own = block(d0 + d1)
        s.gather2 = [remote(own, own, near[d2][1]), remote(own, own, near[d2][3])]
        ends = [block(d0 + d1, d2, hop[d2][3], low), block(d0 + d1, d2, hop[d2][1], high)]
        s.gather3 = [remote(ends[0], ends[0], near[d2][1]), remote(ends[1], ends[1], near[d2][3])]
        s.share = []
        for d in (0, 1, 3, 2):
            ref = block(d0 + d1, d2, hop[d2][d])
            s.share.append(remote(ref, ref, partner))
        pieces.append(s)

    def norm(j):
        loads[j].wait()
        gain1, bias1 = vec[0:1, :], vec[1:2, :]
        for n in range(2):
            mine = layer_norm(xv[4 * j + 2 * core + n].astype(F32), gain1, bias1).astype(BF16)
            ustage[j, 2 * n, core] = mine[:, :256]
            ustage[j, 2 * n + 1, core] = mine[:, 256:]
            theirs = layer_norm(xv[4 * j + 2 * other + n].astype(F32), gain1, bias1).astype(BF16)
            usend[j, 2 * n] = theirs[:, :256]
            usend[j, 2 * n + 1] = theirs[:, 256:]

    def exchange(j, s):
        s.pair.wait_recv()
        start(s.passing)
        start(s.direct)
        uall[j, s.at[0]] = ustage[j, s.at[0]]

    def pass_on(j, s):
        for came, go in zip(s.passing, s.forward):
            came.wait_recv()
            go.start()

    def mix(j, s):
        arrive(s.direct + s.forward)
        u = uall[j].reshape(1024, 256)
        part = jnp.dot(w1t[rings.index(s.axes[0])], u, preferred_element_type=F32)
        hb[j] = part.reshape(4, 4, 16, 256)
        start(s.first + s.straight)

    def sum_q(j, s):
        q = hop[s.axes[1]]
        for i, pos in enumerate((q[1], q[3])):
            s.first[i].wait_recv()
            ref = s.part(pos, i)
            ref[...] = ref[...] + rq[j, i]
            s.second[i].start()

    def start_r(j, s):
        arrive(s.straight + s.second)
        q = co[s.axes[1]]
        hq[j, :, :, low] = s.part(q, 0)[...] + rd[j, 1] + rs[j, 0]
        hq[j, :, :, high] = s.part(q, 1)[...] + rd[j, 0] + rs[j, 1]
        start(s.last)

    def activate(j, s):
        arrive(s.last)
        a, b, c = s.axes
        tile = tile_all[co[c], co[b]]
        total = hq[j, co[c]] + rr[j, 1] + rr[j, 2] + rr[j, 3] + jnp.concatenate([tile, tile], axis=1)
        gall[j, core, s.at[0], s.at[1], s.at[2]] = gelu_of_half(0.5 * total).astype(BF16)
        start(s.gather0)

    def gather1(j, s):
        arrive(s.gather0)
        start(s.gather1)

    def gather2(j, s):
        arrive(s.gather1)
        start(s.gather2)
        s.share[0].start()

    def gather3(j, s):
        for came, go in zip(s.gather2, s.gather3):
            came.wait_recv()
            go.start()
        start(s.share[1:3])

    def share(j, s):
        arrive(s.gather3)
        s.share[3].start()

    def finish(j, s):
        arrive(s.share)

    STEPS = (exchange, pass_on, mix, sum_q, start_r, activate, gather1, gather2, gather3, share, finish)

    def token_half(i, v_ref, mid_ref):
        shift = jnp.concatenate([b2c[...]] * 2, axis=1)
        gain2, bias2 = 0.5 * vec[2:3, :], 0.5 * vec[3:4, :]
        for n in range(2):
            toks = []
            for h in range(2):
                act = gall[i // 2, i % 2, 2 * n + h].reshape(256, 256)
                toks.append(jnp.dot(w2t[...], act, preferred_element_type=F32) + shift)
            mid = (xv[2 * i + n].astype(F32) + jnp.concatenate(toks, axis=1)).astype(BF16)
            mid_ref[128 * n:128 * n + 128, :] = mid
            v_ref[128 * n:128 * n + 128, :] = layer_norm(mid.astype(F32), gain2, bias2).astype(BF16)

    def widen(f, v_ref, pre_ref):
        pre_ref[...] = jnp.dot(v_ref[...], wc1[:, 512 * f:512 * f + 512], preferred_element_type=F32)

    def bend(f, pre_ref, act_ref):
        act_ref[...] = gelu_of_half(pre_ref[...] + 0.5 * bc1[:, 512 * f:512 * f + 512]).astype(BF16)

    def narrow(f, act_ref):
        return jnp.dot(act_ref[...], wc2[512 * f:512 * f + 512, :], preferred_element_type=F32)

    def store(i):
        window = pl.ds(2 * i, 2)
        return local(xv.at[window], z_hbm.at[window], N + 6)

    def end_block(i, mid_ref):
        total = mid_ref[...].astype(F32) + vec[4:5, :] + acc[...] + narrow(3, actb)
        xv[pl.ds(2 * i, 2)] = total.astype(BF16).reshape(2, 128, 512)

    def channel_mix(i, mine, ahead):
        (v_ref, mid_ref), (v_next, mid_next) = mine, ahead
        token_half(jnp.minimum(i + 1, BLOCKS - 1), v_next, mid_next)
        widen(1, v_ref, preb)
        bend(0, prea, acta)
        widen(2, v_ref, prea)
        acc[...] = narrow(0, acta)
        bend(1, preb, actb)
        widen(3, v_ref, preb)
        acc[...] += narrow(1, actb)
        bend(2, prea, acta)
        widen(0, v_next, prea)
        acc[...] += narrow(2, acta)
        bend(3, preb, actb)
        end_block(i, mid_ref)
        store(i).start()

    barrier = pltpu.get_barrier_semaphore()
    peers = group + [near[a][s] for a in "yz" for s in (1, 2, 3)]
    for peer in peers:
        pl.semaphore_signal(barrier, inc=1, device_id={"sp": peer}, device_id_type=MESH)
    start([small[0], loads[0], small[1]])
    start(loads[1:])
    start(small[2:] + large)
    small[0].wait()
    norm(0)
    small[1].wait()
    w1o[...] = w1v[...].T
    pl.semaphore_wait(barrier, len(peers))
    pieces[0].pair.start()
    for a in rings:
        start(w1_ring[a])
    row = lax.broadcasted_iota(jnp.int32, (16, 128), 0)
    tile_in[8] = jnp.where(row == 2 * slot, b1_ref[0], jnp.where(row == 2 * slot + 1, b1_ref[1], 0.0))
    tile_in[slot] = tile_in[8]
    start(b1_group)
    start([w1_mine[a] for a in rings])
    for i, a in enumerate(rings):
        w1t[i, :, lanes(co[a], core)] = w1o[...]
    small[2].wait()
    w2t[...] = w2v[...].T
    b2c[...] = jnp.broadcast_to(vec[5:6, 0:128], (128, 128)).T

    def later_norm(j):
        norm(j)
        pieces[j].pair.start()

    def w1_pass():
        for a in rings:
            for came, go in zip(w1_ring[a], w1_share[a]):
                came.wait_recv()
                go.start()
        arrive(b1_group)
        tile = tile_in[0]
        for n in range(1, 8):
            tile = tile + tile_in[n]
        tile_all[co["z"], co["y"]] = tile
        start(b1_y)

    def w1_end():
        for a in rings:
            arrive([w1_mine[a]] + w1_share[a])
        arrive(b1_y)
        start(b1_z)

    def b1_end():
        arrive(b1_z)

    def run(code):
        n, j = code // 10, code % 10
        if n < len(STEPS):
            STEPS[n](j, pieces[j])
        elif n == NORM:
            later_norm(j)
        else:
            (w1_pass, w1_end, b1_end)[n - W1_PASS]()

    slots = {n: ops for n, ops in enumerate(ORDER) if ops}
    for code in slots.pop(0, ()):
        run(code)
    small[3].wait()
    for load in large:
        load.wait()
    token_half(0, va, mida)
    widen(0, va, prea)

    def loop(p, carry):
        for side, (mine, ahead) in enumerate((((va, mida), (vb, midb)), ((vb, midb), (va, mida)))):
            for n, ops in slots.items():
                if n % 2 == 1 - side:
                    @pl.when(p == (n - 1) // 2)
                    def _():
                        for code in ops:
                            run(code)
            channel_mix(2 * p + side, mine, ahead)
        return carry

    lax.fori_loop(0, BLOCKS // 2, loop, 0)
    local(xv, z_hbm, N + 6).wait()
    for copy in sent:
        copy.wait_send()


RINGS = len({axes[0] for axes, _ in PIECES})
N_COPIES = 31 * N + 7 * RINGS + 7 + 3 + 3


def vmem(*shape, dtype=BF16):
    return pltpu.VMEM(shape, dtype)


def mixer(x, w1, b1, w2, b2, wc1, bc1, wc2, bc2, g1, h1, g2, h2):
    any_space = pl.BlockSpec(memory_space=pl.ANY)
    scalars = pl.BlockSpec(memory_space=pltpu.SMEM)
    rows = [g1, h1, g2, h2, bc2, jnp.pad(b2, (0, 384))]
    return pl.pallas_call(
        mixer_kernel,
        name="mixer",
        out_shape=jax.ShapeDtypeStruct((32, 128, 512), BF16),
        in_specs=[any_space, any_space, scalars] + [any_space] * 5,
        out_specs=any_space,
        scratch_shapes=[
            vmem(32, 128, 512),
            vmem(128, 256),
            vmem(256, 128),
            vmem(8, 512, dtype=F32),
            vmem(1, 2048, dtype=F32),
            vmem(256, 128),
            vmem(RINGS, 256, 1024),
            vmem(128, 256),
            vmem(128, 128, dtype=F32),
            vmem(512, 2048),
            vmem(2048, 512),
            vmem(9, 16, 128, dtype=F32),
            vmem(4, 4, 16, 128, dtype=F32),
            vmem(N, 4, 128, 256),
            vmem(N, 4, 2, 128, 256),
            vmem(N, 4, 2, 128, 256),
            vmem(N, 2, 2, 128, 128),
            vmem(N, 4, 4, 16, 256, dtype=F32),
            vmem(N, 2, 4, 16, 128, dtype=F32),
            vmem(N, 2, 4, 16, 128, dtype=F32),
            vmem(N, 2, 4, 16, 128, dtype=F32),
            vmem(N, 4, 16, 256, dtype=F32),
            vmem(N, 4, 16, 256, dtype=F32),
            vmem(N, 2, 4, 4, 4, 16, 256),
            vmem(256, 512),
            vmem(256, 512),
            vmem(256, 512),
            vmem(256, 512),
            vmem(256, 512, dtype=F32),
            vmem(256, 512, dtype=F32),
            vmem(256, 512),
            vmem(256, 512),
            vmem(256, 512, dtype=F32),
            pltpu.SemaphoreType.DMA((N_COPIES,)),
            pltpu.SemaphoreType.DMA((N_COPIES,)),
            pltpu.SemaphoreType.DMA((N + 7,)),
        ],
        compiler_params=pltpu.CompilerParams(
            collective_id=0, has_side_effects=True, vmem_limit_bytes=60 * 1024 * 1024
        ),
    )(x, w1, b1, w2, jnp.pad(jnp.stack(rows), ((0, 2), (0, 0))), wc1, bc1.reshape(1, 2048), wc2)


def solution(mesh):
    row_spec = P("dp", "sp", None)
    in_specs = (row_spec, P("sp", None), P("sp"), P(None, "sp"), P("sp"), P(None, None), P(None), P(None, None), P(None), P(None), P(None), P(None), P(None))
    return jax.shard_map(mixer, mesh=mesh, in_specs=in_specs, out_specs=row_spec, check_vma=False)
```

time: 102 us -> 96.5 us (0.946)
  Pallas kernels: 97 us -> 89.6 us
  local copies, waits for them, and re-layouts: 4.64 us -> 6.68 us
    pallas_call x1, Pallas kernels: 97 us -> 89.6 us  [mixer(): pl.pallas_call(mixer_kernel, name='mixer', out_shape=jax.ShapeDtypeStruct...]
    pad x0 -> x2, local copies, waits for them, and re-layouts: none -> 1.27 us  [the longest x1 0.66 us: mixer(): rows = [g1, h1, g2, h2, bc2, jnp.pad(b2, (0, 384))]]
where the time goes in v4:
time: 96.5 us; the launch traced here: 96.3 us
  Pallas kernels  89.6 us (93%)
  local copies, waits for them, and re-layouts  6.68 us (7%)
    pallas_call x1, Pallas kernels, mixer(): pl.pallas_call(mixer_kernel, name='mixer', out_shape=jax.ShapeDtypeStruct...  89.6 us
    unnamed x1, local copies, waits for them, and re-layouts  4.64 us

profile of v4, /device:TPU:1, one launch (start us, length us, event | category | flops | bytes accessed | tf_op | source)
XLA Modules:
  0.0 96.3 jit_solution(8737531892287155429)
XLA Ops:
  0.0 0.7 pad.8
  0.7 0.8 stack.27
  1.4 0.6 pad.9.vec_hbm
  2.0 89.6 %mixer.1 = bf16[32,128,512]{2,1,0:T(8,128)(2,1)} custom-call(bf16[32,128,512]{2,1,0:T(8,128)(2,1)} %x_hbm.1, bf16[128,256]{1,0:T(8,128)(2,1)} %w1_hbm.1, f32[2]{0:T(128)} %b1_ref.1, bf16[256,128]{1,0:T(8,128)(2,1)} %w2_hbm.1, f32[8,512]{1,0:T(8,128)} %pad.9.vec_hbm, bf16[512,2048]{1,0:T(8,128)(2,1)} %wc1_hbm.1, f32[1,2048]{1,0:T(1,128)} %bitcast.8, ...), custom_call_target="tpu_custom_call" | custom-call | tf_op jit(solution)/shard_map/mixer/pallas_call | solution.py:395
  91.7 4.6 %copy.15 = bf16[32,128,512]{2,1,0:T(8,128)(2,1)} copy(bf16[32,128,512]{2,1,0:T(8,128)(2,1)} %mixer.1) | data formatting | bytes 8388608

commit v5 on v4

--- a/solution.py
+++ b/solution.py
@@ -10,36 +10,22 @@
 BF16 = jnp.bfloat16
 MESH = pl.DeviceIdType.MESH
 PIECES = (
-    ("zyx", "xyz"),
+    ("zxy", "xzy"),
+    ("yzx", "zyx"),
+    ("xzy", "zxy"),
+    ("xyz", "yxz"),
     ("yzx", "xzy"),
-    ("zxy", "zyx"),
+    ("zxy", "yxz"),
+    ("yzx", "xzy"),
     ("xyz", "zxy"),
-    ("yzx", "yxz"),
-    ("xzy", "yxz"),
-    ("xzy", "zxy"),
-    ("yxz", "xzy"),
 )
 N = len(PIECES)
-NORM, W1_PASS = 11, 12
+NAMES = "abcdefghijk"
 ORDER = (
-    (111, 112, 0, 113, 114, 115, 1, 2, 116, 3, 117, 5, 11, 120, 10, 13, 4, 12, 130, 21, 15, 14, 6, 20, 23, 22, 24,
-     25, 140, 30, 16, 7, 31, 33, 34, 40, 35, 32, 17, 41, 44, 26, 45, 50, 42, 43, 51, 36, 27, 54, 60, 55, 52, 53,
-     61, 46, 37, 64, 70, 62, 63, 65, 47, 56, 71, 74, 72, 73, 80, 57, 66, 75, 81, 84, 82, 83, 90, 67, 91, 100,),
-    (101, 76,),
-    (92, 93, 85,),
-    (102, 103, 94,),
-    (104, 77,),
-    (95, 86,),
-    (105,),
-    (),
-    (87,),
-    (96,),
-    (106,),
-    (97,),
-    (107,),
-    (),
-    (),
-    (),
+    ("n1n2a0n3n4n5a1a2n6a3n7w0b0b1b2a4a5a6v0c0c1b3b5b4", "c2d0b6a7u0d1c3c5e0d2c4b7e1c6d3e2d4d5f0d6e3c7f2e4",
+     "f1e5e6g0d7f3g2g1f4f5f6e7h0g3h2h1g4g5g6f7h3i0h4i1", "i2h6j0g7h5k0",
+    ),
+    "j1i3i4k1", "j2h7", "k2i5", "j3i6", "k3", "j4", "k4j5", "k5i7", "j6", "k6", "", "j7", "k7",
 )
 BLOCKS = 2 * N
 C0 = 0.7978845608028654
@@ -58,8 +44,8 @@
 
 
 def mixer_kernel(
-    x_hbm, w1_hbm, b1_ref, w2_hbm, vec_hbm, wc1_hbm, bc1_hbm, wc2_hbm, z_hbm,
-    xv, w1v, w2v, vec, bc1, w1o, w1t, w2t, b2c, wc1, wc2, tile_in, tile_all, usend, ustage, uall, relay,
+    x_hbm, w1_hbm, b1_ref, w2_hbm, b2_hbm, wc1_hbm, bc1_hbm, wc2_hbm, bc2_hbm, g1_hbm, h1_hbm, g2_hbm, h2_hbm, z_hbm,
+    xv, w1v, w2v, g1, h1, g2, h2, bc2, b2, bc1, w1o, w1t, w2t, b2c, wc1, wc2, tile_in, tile_all, usend, ustage, uall, relay,
     hb, rq, rd, rs, hq, rr, gall, va, vb, mida, midb, prea, preb, acta, actb, acc,
     send_sems, recv_sems, local_sems,
 ):
@@ -99,8 +85,11 @@
         return pltpu.make_async_copy(src, dst, local_sems.at[n])
 
     loads = [local(x_hbm.at[pl.ds(4 * j, 4)], xv.at[pl.ds(4 * j, 4)], j) for j in range(N)]
-    small = [local(vec_hbm, vec, N), local(w1_hbm, w1v, N + 1), local(w2_hbm, w2v, N + 2), local(bc1_hbm, bc1, N + 3)]
-    large = [local(wc1_hbm, wc1, N + 4), local(wc2_hbm, wc2, N + 5)]
+    early = [local(src, dst, N + n) for n, (src, dst) in enumerate(((g1_hbm, g1), (h1_hbm, h1), (w1_hbm, w1v)))]
+    middle = [local(src, dst, N + 3 + n) for n, (src, dst) in enumerate(((w2_hbm, w2v), (b2_hbm, b2)))]
+    late = ((g2_hbm, g2), (h2_hbm, h2), (bc1_hbm, bc1), (bc2_hbm, bc2), (wc1_hbm, wc1), (wc2_hbm, wc2))
+    late = [local(src, dst, N + 5 + n) for n, (src, dst) in enumerate(late)]
+    out_sem = N + 5 + len(late)
 
     def lanes(pos, c):
         return pl.ds(pl.multiple_of((pos * 2 + c) * 128, 128), 128)
@@ -174,7 +163,7 @@
 
     def norm(j):
         loads[j].wait()
-        gain1, bias1 = vec[0:1, :], vec[1:2, :]
+        gain1, bias1 = g1[...], h1[...]
         for n in range(2):
             mine = layer_norm(xv[4 * j + 2 * core + n].astype(F32), gain1, bias1).astype(BF16)
             ustage[j, 2 * n, core] = mine[:, :256]
@@ -250,7 +239,7 @@
 
     def token_half(i, v_ref, mid_ref):
         shift = jnp.concatenate([b2c[...]] * 2, axis=1)
-        gain2, bias2 = 0.5 * vec[2:3, :], 0.5 * vec[3:4, :]
+        gain2, bias2 = 0.5 * g2[...], 0.5 * h2[...]
         for n in range(2):
             toks = []
             for h in range(2):
@@ -271,18 +260,18 @@
 
     def store(i):
         window = pl.ds(2 * i, 2)
-        return local(xv.at[window], z_hbm.at[window], N + 6)
+        return local(xv.at[window], z_hbm.at[window], out_sem)
 
     def end_block(i, mid_ref):
-        total = mid_ref[...].astype(F32) + vec[4:5, :] + acc[...] + narrow(3, actb)
+        total = mid_ref[...].astype(F32) + bc2[...] + acc[...] + narrow(3, actb)
         xv[pl.ds(2 * i, 2)] = total.astype(BF16).reshape(2, 128, 512)
 
     def channel_mix(i, mine, ahead):
         (v_ref, mid_ref), (v_next, mid_next) = mine, ahead
-        token_half(jnp.minimum(i + 1, BLOCKS - 1), v_next, mid_next)
         widen(1, v_ref, preb)
         bend(0, prea, acta)
         widen(2, v_ref, prea)
+        token_half(jnp.minimum(i + 1, BLOCKS - 1), v_next, mid_next)
         acc[...] = narrow(0, acta)
         bend(1, preb, actb)
         widen(3, v_ref, preb)
@@ -298,12 +287,10 @@
     peers = group + [near[a][s] for a in "yz" for s in (1, 2, 3)]
     for peer in peers:
         pl.semaphore_signal(barrier, inc=1, device_id={"sp": peer}, device_id_type=MESH)
-    start([small[0], loads[0], small[1]])
-    start(loads[1:])
-    start(small[2:] + large)
-    small[0].wait()
+    start(early + loads[:1] + middle + loads[1:] + late)
+    for load in early:
+        load.wait()
     norm(0)
-    small[1].wait()
     w1o[...] = w1v[...].T
     pl.semaphore_wait(barrier, len(peers))
     pieces[0].pair.start()
@@ -316,9 +303,10 @@
     start([w1_mine[a] for a in rings])
     for i, a in enumerate(rings):
         w1t[i, :, lanes(co[a], core)] = w1o[...]
-    small[2].wait()
+    for load in middle:
+        load.wait()
     w2t[...] = w2v[...].T
-    b2c[...] = jnp.broadcast_to(vec[5:6, 0:128], (128, 128)).T
+    b2c[...] = jnp.broadcast_to(b2[...], (128, 128)).T
 
     def later_norm(j):
         norm(j)
@@ -345,20 +333,18 @@
     def b1_end():
         arrive(b1_z)
 
-    def run(code):
-        n, j = code // 10, code % 10
-        if n < len(STEPS):
-            STEPS[n](j, pieces[j])
-        elif n == NORM:
-            later_norm(j)
-        else:
-            (w1_pass, w1_end, b1_end)[n - W1_PASS]()
+    def run(ops):
+        for n, j in zip(ops[::2], ops[1::2]):
+            j = int(j)
+            if n in NAMES:
+                STEPS[NAMES.index(n)](j, pieces[j])
+            else:
+                {"n": lambda: later_norm(j), "w": w1_pass, "v": w1_end, "u": b1_end}[n]()
 
     slots = {n: ops for n, ops in enumerate(ORDER) if ops}
-    for code in slots.pop(0, ()):
-        run(code)
-    small[3].wait()
-    for load in large:
+    for ops in slots.pop(0):
+        run(ops)
+    for load in late:
         load.wait()
     token_half(0, va, mida)
     widen(0, va, prea)
@@ -368,14 +354,13 @@
             for n, ops in slots.items():
                 if n % 2 == 1 - side:
                     @pl.when(p == (n - 1) // 2)
-                    def _():
-                        for code in ops:
-                            run(code)
+                    def _(ops=ops):
+                        run(ops)
             channel_mix(2 * p + side, mine, ahead)
         return carry
 
     lax.fori_loop(0, BLOCKS // 2, loop, 0)
-    local(xv, z_hbm, N + 6).wait()
+    local(xv, z_hbm, out_sem).wait()
     for copy in sent:
         copy.wait_send()
 
@@ -391,18 +376,18 @@
 def mixer(x, w1, b1, w2, b2, wc1, bc1, wc2, bc2, g1, h1, g2, h2):
     any_space = pl.BlockSpec(memory_space=pl.ANY)
     scalars = pl.BlockSpec(memory_space=pltpu.SMEM)
-    rows = [g1, h1, g2, h2, bc2, jnp.pad(b2, (0, 384))]
     return pl.pallas_call(
         mixer_kernel,
         name="mixer",
         out_shape=jax.ShapeDtypeStruct((32, 128, 512), BF16),
-        in_specs=[any_space, any_space, scalars] + [any_space] * 5,
+        in_specs=[any_space, any_space, scalars] + [any_space] * 10,
         out_specs=any_space,
         scratch_shapes=[
             vmem(32, 128, 512),
             vmem(128, 256),
             vmem(256, 128),
-            vmem(8, 512, dtype=F32),
+            *[vmem(1, 512, dtype=F32)] * 5,
+            vmem(1, 128, dtype=F32),
             vmem(1, 2048, dtype=F32),
             vmem(256, 128),
             vmem(RINGS, 256, 1024),
@@ -434,12 +419,12 @@
             vmem(256, 512, dtype=F32),
             pltpu.SemaphoreType.DMA((N_COPIES,)),
             pltpu.SemaphoreType.DMA((N_COPIES,)),
-            pltpu.SemaphoreType.DMA((N + 7,)),
+            pltpu.SemaphoreType.DMA((N + 12,)),
         ],
         compiler_params=pltpu.CompilerParams(
             collective_id=0, has_side_effects=True, vmem_limit_bytes=60 * 1024 * 1024
         ),
-    )(x, w1, b1, w2, jnp.pad(jnp.stack(rows), ((0, 2), (0, 0))), wc1, bc1.reshape(1, 2048), wc2)
+    )(x, w1, b1, w2, *(v.reshape(1, -1) if v.ndim == 1 else v for v in (b2, wc1, bc1, wc2, bc2, g1, h1, g2, h2)))
 
 
 def solution(mesh):

time: 96.5 us -> 93.3 us (0.967)
  local copies, waits for them, and re-layouts: 6.68 us -> 4.64 us
  Pallas kernels: 89.6 us -> 88.5 us
    pad x2 -> x0, local copies, waits for them, and re-layouts: 1.27 us -> none  [the longest x1 0.66 us: mixer(): rows = [g1, h1, g2, h2, bc2, jnp.pad(b2, (0, 384))]]
    pallas_call x1, Pallas kernels: 89.6 us -> 88.5 us  [mixer(): pl.pallas_call(mixer_kernel, name='mixer', out_shape=jax.ShapeDtypeStruct...]
where the time goes in v5:
time: 93.3 us; the launch traced here: 93.1 us
  Pallas kernels  88.5 us (95%)
  local copies, waits for them, and re-layouts  4.64 us (5%)
    pallas_call x1, Pallas kernels, mixer(): pl.pallas_call(mixer_kernel, name='mixer', out_shape=jax.ShapeDtypeStruct...  88.5 us
    unnamed x1, local copies, waits for them, and re-layouts  4.64 us

profile of v5, /device:TPU:1, one launch (start us, length us, event | category | flops | bytes accessed | tf_op | source)
XLA Modules:
  0.0 93.1 jit_solution(9037495982423015759)
XLA Ops:
  0.0 88.5 %mixer.1 = bf16[32,128,512]{2,1,0:T(8,128)(2,1)} custom-call(bf16[32,128,512]{2,1,0:T(8,128)(2,1)} %x_hbm.1, bf16[128,256]{1,0:T(8,128)(2,1)} %w1_hbm.1, f32[2]{0:T(128)} %b1_ref.1, bf16[256,128]{1,0:T(8,128)(2,1)} %w2_hbm.1, f32[1,128]{1,0:T(1,128)} %bitcast.13, bf16[512,2048]{1,0:T(8,128)(2,1)} %wc1_hbm.1, f32[1,2048]{1,0:T(1,128)} %bitcast.7, ...), custom_call_target="tpu_custom_call" | custom-call | tf_op jit(solution)/shard_map/mixer/pallas_call | solution.py:379
  88.5 4.6 %copy.15 = bf16[32,128,512]{2,1,0:T(8,128)(2,1)} copy(bf16[32,128,512]{2,1,0:T(8,128)(2,1)} %mixer.1) | data formatting | bytes 8388608
